TPU v7x, 32 devices: a whole 2x2x4 slice. The times are simulated.
32 devices in a mesh: row: 4 (over y, core), col: 8 (over z, x).
Axes of the slice: x: 2, y: 2, z: 4, core: 2. Of those that a mesh axis runs over, the one named last changes fastest.
Arguments:
- phase: float32 [512, 32, 512], P('col', 'row'), may hold values from -6 to 6
- velocity: float32 [3, 512, 32, 512], P(None, 'col', 'row'), may hold values from -12 to 12
Outputs:
- phase_next: float32 [512, 32, 512], P('col', 'row')
- velocity_next: float32 [3, 512, 32, 512], P(None, 'col', 'row')
All inputs are finite; a program needn't handle non-finite values.
Results may differ from a plain program's by a relative error of at most 0.013.
Values may be sent and summed in bfloat16 or wider, within the bound.
A program may use at most 128 MiB of HBM per device.

v0:
```python
import math

import jax
import jax.numpy as jnp
from jax import lax
from jax.sharding import PartitionSpec as P

NX = 512
NY = 512
KC = 192
KY = 384


time_step = 0.001
epsilon = 0.01
mobility = 1.0
reynolds = 100.0
stabilizer = 2.0


def cos_sin(row_index, col_index, period):
    residue = row_index[:, None] * col_index[None, :] % period
    angles = residue.astype(jnp.float32) * (2.0 * math.pi / period)
    return jnp.stack([jnp.cos(angles), jnp.sin(angles)]).astype(jnp.bfloat16)


def pair_sum(pieces, direction, stack_axis):
    if direction < 0:
        real_part = pieces[0, 0] + pieces[1, 1]
        imag_part = pieces[1, 0] - pieces[0, 1]
    else:
        real_part = pieces[0, 0] - pieces[1, 1]
        imag_part = pieces[0, 1] + pieces[1, 0]
    return jnp.stack([real_part, imag_part], axis=stack_axis)


def times_i(values):
    return jnp.stack([-values[:, 1], values[:, 0]], axis=1)


def phase_terms(phase, velocity, gradient, lap_field):
    advect = velocity[0] * gradient[0] + velocity[1] * gradient[1] + velocity[2] * gradient[2]
    bulk_term = phase * phase * phase - phase
    potential = bulk_term - epsilon * epsilon * lap_field
    return (advect, bulk_term, potential)


def momentum(velocity, vortex, gradient, potential):
    return jnp.stack(
        [
            velocity[1] * vortex[2] - velocity[2] * vortex[1] + potential * gradient[0],
            velocity[2] * vortex[0] - velocity[0] * vortex[2] + potential * gradient[1],
            velocity[0] * vortex[1] - velocity[1] * vortex[0] + potential * gradient[2],
        ]
    )


def on_device(phase, velocity):
    col_count = lax.axis_size("col")
    row_count = lax.axis_size("row")
    rows_y = phase.shape[0]
    planes = phase.shape[1]
    total_z = planes * row_count
    half_z = 3 * total_z // 8
    modes_z = 2 * half_z
    kx_local = KC // col_count
    ky_local = KY // row_count
    scale_inv = 1.0 / (NX * NY * total_z)
    table_x = cos_sin(jnp.arange(NX, dtype=jnp.int32), jnp.arange(KC, dtype=jnp.int32), NX)
    table_y = cos_sin(jnp.arange(NY, dtype=jnp.int32), jnp.arange(KY, dtype=jnp.int32) - KC, NY)
    table_z = cos_sin(
        jnp.arange(total_z, dtype=jnp.int32), jnp.arange(modes_z, dtype=jnp.int32) - half_z, total_z
    )
    y_forward = table_y.reshape(2, col_count, rows_y, KY)
    y_inverse = table_y.reshape(2, col_count, rows_y, row_count, ky_local)
    z_table = table_z.reshape(2, row_count, planes, modes_z)
    weight = jnp.where(jnp.arange(KC) == 0, 1.0, 2.0).astype(jnp.bfloat16)[:, None, None, None]

    def along_y(incoming):
        field_count = incoming.shape[1]
        shaped = incoming.reshape(incoming.shape[0], field_count, col_count, 2, rows_y, planes)
        pieces = jnp.einsum(
            "afcpyz,tcyb->ptafbz", shaped, y_forward, preferred_element_type=jnp.float32
        )
        joined = pair_sum(pieces, -1, 2).astype(jnp.bfloat16)
        return joined.reshape(incoming.shape[0], field_count, 2, KY * planes)

    def along_z(incoming):
        field_count = incoming.shape[1]
        shaped = incoming.reshape(incoming.shape[0], field_count, 2, row_count, ky_local, planes)
        pieces = jnp.einsum(
            "afprbz,trzm->ptafbm", shaped, z_table, preferred_element_type=jnp.float32
        )
        joined = pair_sum(pieces, -1, 2) * scale_inv
        return joined.reshape(incoming.shape[0], field_count, 2, ky_local * modes_z)

    def back_y(incoming):
        field_count = incoming.shape[1]
        shaped = incoming.reshape(incoming.shape[0], field_count, 2, row_count, planes, ky_local)
        pieces = jnp.einsum(
            "afprzb,tcyrb->ptafcyz", shaped, y_inverse, preferred_element_type=jnp.float32
        )
        joined = pair_sum(pieces, 1, 3).astype(jnp.bfloat16)
        return joined.reshape(incoming.shape[0], field_count, col_count * 2 * rows_y * planes)

    def back_x(incoming):
        field_count = incoming.shape[1]
        shaped = incoming.reshape(KC, field_count, 2, rows_y, planes)
        scaled = jnp.stack([shaped[:, :, 0] * weight, -(shaped[:, :, 1] * weight)], axis=2)
        return jnp.einsum("afpyz,pxa->fyzx", scaled, table_x, preferred_element_type=jnp.float32)

    def forward(fields):
        field_count = fields.shape[0]
        pieces = jnp.einsum(
            "fyzx,txa->tafyz",
            fields.astype(jnp.bfloat16),
            table_x,
            preferred_element_type=jnp.float32,
        )
        x_lines = jnp.stack([pieces[0], -pieces[1]], axis=2).astype(jnp.bfloat16)
        x_lines = x_lines.reshape(KC, field_count, 2 * rows_y * planes)
        spread = along_y(lax.all_to_all(x_lines, "col", split_axis=0, concat_axis=2, tiled=True))
        return along_z(lax.all_to_all(spread, "row", split_axis=3, concat_axis=3, tiled=True))

    def inverse(spectra):
        field_count = spectra.shape[1]
        shaped = spectra.astype(jnp.bfloat16).reshape(kx_local, field_count, 2, ky_local, modes_z)
        pieces = jnp.einsum(
            "afpbm,trzm->ptafrzb", shaped, z_table, preferred_element_type=jnp.float32
        )
        z_planes = (
            pair_sum(pieces, 1, 2)
            .astype(jnp.bfloat16)
            .reshape(kx_local, field_count, 2, total_z * ky_local)
        )
        spread = back_y(lax.all_to_all(z_planes, "row", split_axis=3, concat_axis=3, tiled=True))
        return back_x(lax.all_to_all(spread, "col", split_axis=2, concat_axis=0, tiled=True))

    spectra = forward(jnp.concatenate([phase[None], velocity], axis=0))
    wave_x = (lax.axis_index("col") * kx_local + jnp.arange(kx_local, dtype=jnp.int32)).astype(
        jnp.float32
    )[:, None, None]
    modes_y = lax.axis_index("row") * ky_local + jnp.arange(ky_local, dtype=jnp.int32) - KC
    wave_y = jnp.broadcast_to(modes_y.astype(jnp.float32)[:, None], (ky_local, modes_z)).reshape(-1)
    z_values = (jnp.arange(modes_z, dtype=jnp.int32) - half_z).astype(jnp.float32) * (NX / total_z)
    wave_z = jnp.broadcast_to(z_values[None, :], (ky_local, modes_z)).reshape(-1)
    squared = wave_x * wave_x + wave_y * wave_y + wave_z * wave_z
    coeff_phase = spectra[:, 0]
    coeff_u = spectra[:, 1]
    coeff_v = spectra[:, 2]
    coeff_w = spectra[:, 3]
    gradients = [
        times_i(wave_x * coeff_phase),
        times_i(wave_y * coeff_phase),
        times_i(wave_z * coeff_phase),
    ]
    laplace = -squared * coeff_phase
    vortex_hat = [
        times_i(wave_y * coeff_w - wave_z * coeff_v),
        times_i(wave_z * coeff_u - wave_x * coeff_w),
        times_i(wave_x * coeff_v - wave_y * coeff_u),
    ]
    leading = inverse(jnp.stack(gradients + [laplace], axis=1))
    advect, bulk_term, potential = phase_terms(phase, velocity, leading[0:3], leading[3])
    phase_side = forward(jnp.stack([advect, bulk_term]))
    vortex = inverse(jnp.stack(vortex_hat, axis=1))
    flow_side = forward(momentum(velocity, vortex, leading[0:3], potential))
    nonlinear = jnp.concatenate([phase_side, flow_side], axis=1)
    mean_mode = (wave_x == 0) & (wave_y == 0) & (wave_z == 0)
    advect_hat = jnp.where(mean_mode, 0.0, nonlinear[:, 0])
    bulk_hat = nonlinear[:, 1]
    stable_part = 1.0 / time_step + mobility * stabilizer * squared
    new_phase = (stable_part * coeff_phase - advect_hat - mobility * squared * bulk_hat) / (
        stable_part + mobility * epsilon * epsilon * squared * squared
    )
    viscous = 1.0 / time_step + squared / reynolds
    unprojected = [
        (spectra[:, 1 + j] / time_step + nonlinear[:, 2 + j]) / viscous for j in range(3)
    ]
    normal_part = (
        wave_x * unprojected[0] + wave_y * unprojected[1] + wave_z * unprojected[2]
    ) / jnp.maximum(squared, 1.0)
    waves = [wave_x, wave_y, wave_z]
    new_flow = [unprojected[j] - waves[j] * normal_part for j in range(3)]
    result = inverse(jnp.stack([new_phase] + new_flow, axis=1))
    return (result[0], result[1:4])


def solution(mesh):
    return jax.shard_map(
        on_device,
        mesh=mesh,
        in_specs=(P("col", "row", None), P(None, "col", "row", None)),
        out_specs=(P("col", "row", None), P(None, "col", "row", None)),
        check_vma=False,
    )
```

profile of v0, /device:TPU:0, one launch (start us, length us, event | category | flops | bytes accessed | tf_op | source)
XLA Modules:
  0.0 845.1 jit_solution(9600123166907076406)
XLA Ops:
  31.2 26.8 %all-to-all-done = bf16[192,4,1024]{2,1,0:T(4,128)(2,1)S(1)} async-done(((bf16[192,4,1024]{2,1,0:T(4,128)(2,1)}), bf16[192,4,1024]{2,1,0:T(4,128)(2,1)S(1)}, u32[]{:S(2)}, u32[]{:S(2)}) %all-to-all-start) | async-done | bytes 1572896 | tf_op jit(solution)/shard_map/all_to_all | solution.py:122
  87.2 25.2 %copy.564 = bf16[24,4,2,3072]{0,1,2,3:T(4,128)(2,1)} copy(bf16[24,4,2,3072]{0,3,1,2:T(8,128)(2,1)S(1)} %pad_maximum_fusion) | data formatting | bytes 2359296 | tf_op jit(solution)/shard_map/stack | solution.py:34
  112.4 10.7 %reshape.1359 = bf16[4,2,73728]{2,1,0:T(2,128)(2,1)} reshape(bf16[3072,2,4,24]{3,2,1,0:T(4,128)(2,1)} %bitcast.532) | data formatting | bytes 2359296
  128.0 14.4 %all-to-all-done.1 = bf16[4,2,73728]{2,1,0:T(2,128)(2,1)S(1)} async-done(((bf16[4,2,73728]{2,1,0:T(2,128)(2,1)}), bf16[4,2,73728]{2,1,0:T(2,128)(2,1)S(1)}, u32[]{:S(2)}, u32[]{:S(2)}) %all-to-all-start.1) | async-done | bytes 1179680 | tf_op jit(solution)/shard_map/all_to_all | solution.py:123
  142.4 10.2 %reshape.1360 = bf16[3072,2,4,24]{3,2,1,0:T(4,128)(2,1)} reshape(bf16[4,2,73728]{2,1,0:T(2,128)(2,1)S(1)} %all-to-all-done.1) | data formatting | bytes 2359296
  152.6 9.8 %copy.383 = bf16[24,4,2,4,96,8]{4,5,3,2,1,0:T(8,128)(2,1)S(1)} copy(bf16[24,4,2,4,96,8]{0,1,2,5,4,3:T(4,128)(2,1)} %bitcast.538) | data formatting | bytes 2359296 | tf_op jit(solution)/shard_map/reshape | solution.py:90
  230.2 10.3 %reshape.1361 = bf16[4,2,73728]{2,1,0:T(2,128)(2,1)} reshape(bf16[3072,2,4,24]{3,2,1,0:T(4,128)(2,1)} %bitcast.533) | data formatting | bytes 2359296
  263.9 10.5 %copy.562 = bf16[24,3,8192]{0,1,2:T(4,128)(2,1)} copy(bf16[24,3,8192]{0,2,1:T(8,128)(2,1)} %bitcast.534) | data formatting | bytes 2359296 | tf_op jit(solution)/shard_map/convert_element_type | solution.py:103
  274.4 10.9 %reshape.1367 = bf16[8,2,36864]{2,1,0:T(2,128)(2,1)} reshape(bf16[8192,3,24]{2,1,0:T(4,128)(2,1)} %bitcast.521) | data formatting | bytes 2359296
  289.8 10.2 %reshape.1362 = bf16[3072,2,4,24]{3,2,1,0:T(4,128)(2,1)} reshape(bf16[4,2,73728]{2,1,0:T(2,128)(2,1)S(1)} %all-to-all-done.2) | data formatting | bytes 2359296
  315.5 12.2 %copy.563 = bf16[24,4,8192]{0,1,2:T(4,128)(2,1)} copy(bf16[24,4,8192]{0,2,1:T(8,128)(2,1)} %bitcast.526) | data formatting | bytes 3145728 | tf_op jit(solution)/shard_map/convert_element_type | solution.py:103
  327.7 12.6 %reshape.1363 = bf16[8,2,49152]{2,1,0:T(2,128)(2,1)} reshape(bf16[8192,4,24]{2,1,0:T(4,128)(2,1)} %bitcast.527) | data formatting | bytes 3145728
  346.6 11.4 %reshape.1368 = bf16[8192,3,24]{2,1,0:T(4,128)(2,1)} reshape(bf16[8,2,36864]{2,1,0:T(2,128)(2,1)} %all-to-all-done.7) | data formatting | bytes 2359296
  358.0 11.2 %copy.559 = bf16[24,3,8,1024]{0,2,3,1:T(8,128)(2,1)} copy(bf16[24,3,8,1024]{0,1,3,2:T(4,128)(2,1)} %bitcast.522) | data formatting | bytes 2359296 | tf_op jit(solution)/shard_map/all_to_all | solution.py:137
  383.9 13.1 %reshape.1364 = bf16[8192,4,24]{2,1,0:T(4,128)(2,1)} reshape(bf16[8,2,49152]{2,1,0:T(2,128)(2,1)S(1)} %all-to-all-done.3) | data formatting | bytes 3145728
  397.0 12.1 %copy.558 = bf16[24,4,8,1024]{0,2,3,1:T(8,128)(2,1)} copy(bf16[24,4,8,1024]{0,1,3,2:T(4,128)(2,1)} %bitcast.528) | data formatting | bytes 3145728 | tf_op jit(solution)/shard_map/all_to_all | solution.py:137
  409.1 10.1 %reshape.1319 = bf16[192,4,2,64,8]{0,4,3,2,1:T(8,128)(2,1)S(1)} reshape(bf16[8,24,4,1024]{1,0,3,2:T(8,128)(2,1)} %bitcast.523) | data formatting | bytes 3145728 | tf_op jit(solution)/shard_map/reshape | solution.py:108
  435.6 17.4 %all-to-all-done.4 = bf16[192,2,1024]{2,1,0:T(2,128)(2,1)S(1)} async-done(((bf16[192,2,1024]{2,1,0:T(2,128)(2,1)}), bf16[192,2,1024]{2,1,0:T(2,128)(2,1)S(1)}, u32[]{:S(2)}, u32[]{:S(2)}) %all-to-all-start.4) | async-done | bytes 786464 | tf_op jit(solution)/shard_map/all_to_all | solution.py:122
  464.9 19.1 %copy.566 = bf16[24,2,2,3072]{0,1,2,3:T(2,128)(2,1)S(1)} copy(bf16[24,2,2,3072]{0,3,1,2:T(8,128)(2,1)S(1)} %pad_maximum_fusion.3) | data formatting | bytes 1179648 | tf_op jit(solution)/shard_map/stack | solution.py:34
  526.8 16.3 %all-to-all-done.8 = bf16[192,3,1024]{2,1,0:T(4,128)(2,1)} async-done(((bf16[192,3,1024]{2,1,0:T(4,128)(2,1)}), bf16[192,3,1024]{2,1,0:T(4,128)(2,1)}, u32[]{:S(2)}, u32[]{:S(2)}) %all-to-all-start.8) | async-done | bytes 1179680 | tf_op jit(solution)/shard_map/all_to_all | solution.py:122
  568.7 42.6 %copy.565 = bf16[24,3,2,3072]{0,2,1,3:T(2,128)(2,1)} copy(bf16[24,3,2,3072]{0,3,1,2:T(8,128)(2,1)S(1)} %pad_maximum_fusion.1) | data formatting | bytes 1769472 | tf_op jit(solution)/shard_map/stack | solution.py:34
  636.9 8.7 %reshape.1370 = bf16[3072,3,2,24]{3,2,1,0:T(2,128)(2,1)} reshape(bf16[4,2,55296]{2,1,0:T(2,128)(2,1)} %all-to-all-done.9) | data formatting | bytes 1769472
  645.6 9.0 %copy.445 = bf16[24,3,2,4,96,8]{4,5,3,2,1,0:T(8,128)(2,1)S(1)} copy(bf16[24,3,2,4,96,8]{0,2,1,5,4,3:T(2,128)(2,1)} %bitcast.540) | data formatting | bytes 1769472 | tf_op jit(solution)/shard_map/reshape | solution.py:90
  686.5 9.7 %reshape.1373 = bf16[4,2,73728]{2,1,0:T(2,128)(2,1)S(1)} reshape(bf16[3072,2,4,24]{3,2,1,0:T(4,128)(2,1)} %bitcast.537) | data formatting | bytes 2359296
  696.2 18.3 %all_to_all.120 = bf16[4,2,73728]{2,1,0:T(2,128)(2,1)S(1)} all-to-all(bf16[4,2,73728]{2,1,0:T(2,128)(2,1)S(1)} %reshape.1373), channel_id=1, replica_groups=mesh['row'=4,'col'=8] {'row'}, dimensions={0} | all-to-all | bytes 2359296 | tf_op jit(solution)/shard_map/all_to_all | solution.py:136
  714.5 10.2 %reshape.1374 = bf16[3072,2,4,24]{3,2,1,0:T(4,128)(2,1)} reshape(bf16[4,2,73728]{2,1,0:T(2,128)(2,1)S(1)} %all_to_all.120) | data formatting | bytes 2359296
  740.3 12.2 %copy.561 = bf16[24,4,8192]{0,1,2:T(4,128)(2,1)} copy(bf16[24,4,8192]{0,2,1:T(8,128)(2,1)} %bitcast.529) | data formatting | bytes 3145728 | tf_op jit(solution)/shard_map/convert_element_type | solution.py:103
  752.4 11.9 %reshape.1375 = bf16[8,2,49152]{2,1,0:T(2,128)(2,1)S(1)} reshape(bf16[8192,4,24]{2,1,0:T(4,128)(2,1)} %bitcast.530) | data formatting | bytes 3145728
  764.4 40.3 %all_to_all.121 = bf16[8,2,49152]{2,1,0:T(2,128)(2,1)S(1)} all-to-all(bf16[8,2,49152]{2,1,0:T(2,128)(2,1)S(1)} %reshape.1375), channel_id=1, replica_groups=mesh['row'=4,'col'=8] {'col'}, dimensions={0} | all-to-all | bytes 3145728 | tf_op jit(solution)/shard_map/all_to_all | solution.py:137
  804.7 12.9 %reshape.1376 = bf16[8192,4,24]{2,1,0:T(4,128)(2,1)} reshape(bf16[8,2,49152]{2,1,0:T(2,128)(2,1)S(1)} %all_to_all.121) | data formatting | bytes 3145728
  817.6 12.1 %copy.557 = bf16[24,4,8,1024]{0,2,3,1:T(8,128)(2,1)} copy(bf16[24,4,8,1024]{0,1,3,2:T(4,128)(2,1)} %bitcast.531) | data formatting | bytes 3145728 | tf_op jit(solution)/shard_map/all_to_all | solution.py:137
  829.7 9.6 %reshape.1327 = bf16[192,4,2,64,8]{0,4,3,2,1:T(8,128)(2,1)S(1)} reshape(bf16[8,24,4,1024]{1,0,3,2:T(8,128)(2,1)} %bitcast.524) | data formatting | bytes 3145728 | tf_op jit(solution)/shard_map/reshape | solution.py:108
  (288 shorter events, 370.3 us)
Async XLA Ops:
  2.3 5.5 copy-start.4
  2.3 5.5 copy-start.7
  13.6 44.5 %all-to-all-start = ((bf16[192,4,1024]{2,1,0:T(4,128)(2,1)}), bf16[192,4,1024]{2,1,0:T(4,128)(2,1)S(1)}, u32[]{:S(2)}, u32[]{:S(2)}) async-start(bf16[192,4,1024]{2,1,0:T(4,128)(2,1)} %copy.375), calls=%async_computation | async-start | bytes 3145728 | tf_op jit(solution)/shard_map/all_to_all | solution.py:122
  21.3 198.4 %copy-start.27 = (bf16[1,4,8,24]{3,2,1,0:T(8,128)(2,1)}, bf16[1,4,8,24]{3,2,1,0:T(8,128)(2,1)S(1)}, u32[]{:S(2)}) copy-start(bf16[1,4,8,24]{3,2,1,0:T(8,128)(2,1)S(1)} %get-tuple-element.50) | copy-start | bytes 4612
  21.3 198.4 %copy-start.31 = (bf16[1,4,8,24]{3,2,1,0:T(8,128)(2,1)}, bf16[1,4,8,24]{3,2,1,0:T(8,128)(2,1)S(1)}, u32[]{:S(2)}) copy-start(bf16[1,4,8,24]{3,2,1,0:T(8,128)(2,1)S(1)} %get-tuple-element.51) | copy-start | bytes 4612
  123.1 19.3 %all-to-all-start.1 = ((bf16[4,2,73728]{2,1,0:T(2,128)(2,1)}), bf16[4,2,73728]{2,1,0:T(2,128)(2,1)S(1)}, u32[]{:S(2)}, u32[]{:S(2)}) async-start(bf16[4,2,73728]{2,1,0:T(2,128)(2,1)} %reshape.1359), calls=%async_computation.1 | async-start | bytes 2359296 | tf_op jit(solution)/shard_map/all_to_all | solution.py:123
  126.6 51.7 %copy-start.38 = (f32[24]{0:T(128)}, f32[24]{0:T(128)S(1)}, u32[]{:S(2)}) copy-start(f32[24]{0:T(128)S(1)} %add_convert_fusion.2) | copy-start | bytes 292
  126.9 51.4 %copy-start.18 = (f32[2304]{0:T(1024)}, f32[2304]{0:T(1024)S(1)}, u32[]{:S(2)}) copy-start(f32[2304]{0:T(1024)S(1)} %reshape.1314) | copy-start | bytes 27652
  215.9 24.5 %all-to-all-start.6 = ((bf16[4,2,55296]{2,1,0:T(2,128)(2,1)}), bf16[4,2,55296]{2,1,0:T(2,128)(2,1)S(1)}, u32[]{:S(2)}, u32[]{:S(2)}) async-start(bf16[4,2,55296]{2,1,0:T(2,128)(2,1)} %reshape.1365), calls=%async_computation.6 | async-start | bytes 1769472 | tf_op jit(solution)/shard_map/all_to_all | solution.py:136
  240.5 44.9 %all-to-all-start.2 = ((bf16[4,2,73728]{2,1,0:T(2,128)(2,1)}), bf16[4,2,73728]{2,1,0:T(2,128)(2,1)S(1)}, u32[]{:S(2)}, u32[]{:S(2)}) async-start(bf16[4,2,73728]{2,1,0:T(2,128)(2,1)} %reshape.1361), calls=%async_computation.2 | async-start | bytes 2359296 | tf_op jit(solution)/shard_map/all_to_all | solution.py:136
  244.5 7.8 copy-start.21
  244.5 7.8 copy-start.24
  285.3 55.0 %all-to-all-start.7 = ((bf16[8,2,36864]{2,1,0:T(2,128)(2,1)}), bf16[8,2,36864]{2,1,0:T(2,128)(2,1)}, u32[]{:S(2)}, u32[]{:S(2)}) async-start(bf16[8,2,36864]{2,1,0:T(2,128)(2,1)} %reshape.1367), calls=%async_computation.7 | async-start | bytes 2359296 | tf_op jit(solution)/shard_map/all_to_all | solution.py:137
  289.8 10.2 %copy-start.22 = (bf16[1,8,64,4,96]{4,2,3,1,0:T(8,128)(2,1)S(1)}, bf16[1,8,64,4,96]{4,2,3,1,0:T(8,128)(2,1)}, u32[]{:S(2)}) copy-start(bf16[1,8,64,4,96]{4,2,3,1,0:T(8,128)(2,1)} %get-tuple-element.46) | copy-start | bytes 1179652
  289.8 10.2 %copy-start.25 = (bf16[1,8,64,4,96]{4,2,3,1,0:T(8,128)(2,1)S(1)}, bf16[1,8,64,4,96]{4,2,3,1,0:T(8,128)(2,1)}, u32[]{:S(2)}) copy-start(bf16[1,8,64,4,96]{4,2,3,1,0:T(8,128)(2,1)} %get-tuple-element.47) | copy-start | bytes 1179652
  340.4 43.5 %all-to-all-start.3 = ((bf16[8,2,49152]{2,1,0:T(2,128)(2,1)}), bf16[8,2,49152]{2,1,0:T(2,128)(2,1)S(1)}, u32[]{:S(2)}, u32[]{:S(2)}) async-start(bf16[8,2,49152]{2,1,0:T(2,128)(2,1)} %reshape.1363), calls=%async_computation.3 | async-start | bytes 3145728 | tf_op jit(solution)/shard_map/all_to_all | solution.py:137
  428.9 24.2 %all-to-all-start.4 = ((bf16[192,2,1024]{2,1,0:T(2,128)(2,1)}), bf16[192,2,1024]{2,1,0:T(2,128)(2,1)S(1)}, u32[]{:S(2)}, u32[]{:S(2)}) async-start(bf16[192,2,1024]{2,1,0:T(2,128)(2,1)} %copy.405), calls=%async_computation.4 | async-start | bytes 1572864 | tf_op jit(solution)/shard_map/all_to_all | solution.py:122
  488.7 13.0 %all-to-all-start.5 = ((bf16[4,2,36864]{2,1,0:T(2,128)(2,1)}), bf16[4,2,36864]{2,1,0:T(2,128)(2,1)S(1)}, u32[]{:S(2)}, u32[]{:S(2)}) async-start(bf16[4,2,36864]{2,1,0:T(2,128)(2,1)} %reshape.1371), calls=%async_computation.5 | async-start | bytes 1179648 | tf_op jit(solution)/shard_map/all_to_all | solution.py:123
  498.9 7.3 copy-start.19
  501.6 41.5 %all-to-all-start.8 = ((bf16[192,3,1024]{2,1,0:T(4,128)(2,1)}), bf16[192,3,1024]{2,1,0:T(4,128)(2,1)}, u32[]{:S(2)}, u32[]{:S(2)}) async-start(bf16[192,3,1024]{2,1,0:T(4,128)(2,1)} %copy.437), calls=%async_computation.8 | async-start | bytes 3145728 | tf_op jit(solution)/shard_map/all_to_all | solution.py:122
  512.2 5.9 copy-start.28
  512.2 5.9 copy-start.32
  611.3 12.9 %copy-start.2 = (f32[24,4,2,2304]{3,0,1,2:T(8,128)S(1)}, f32[24,4,2,2304]{3,0,1,2:T(8,128)}, u32[]{:S(2)}) copy-start(f32[24,4,2,2304]{3,0,1,2:T(8,128)} %copy-done.1) | copy-start | bytes 5308420
  611.3 12.9 %copy-start.14 = (f32[24,2304]{1,0:T(8,128)S(1)}, f32[24,2304]{1,0:T(8,128)}, u32[]{:S(2)}) copy-start(f32[24,2304]{1,0:T(8,128)} %get-tuple-element.40) | copy-start | bytes 663556
  611.3 12.9 %copy-start.15 = (f32[24,2304]{1,0:T(8,128)S(1)}, f32[24,2304]{1,0:T(8,128)}, u32[]{:S(2)}) copy-start(f32[24,2304]{1,0:T(8,128)} %get-tuple-element.42) | copy-start | bytes 663556
  611.3 12.9 %copy-start.16 = (f32[24,2304]{1,0:T(8,128)S(1)}, f32[24,2304]{1,0:T(8,128)}, u32[]{:S(2)}) copy-start(f32[24,2304]{1,0:T(8,128)} %get-tuple-element.45) | copy-start | bytes 663556
  611.3 12.9 %copy-start.37 = (pred[24,2304]{1,0:T(8,128)(4,1)S(1)}, pred[24,2304]{1,0:T(8,128)(4,1)}, u32[]{:S(2)}) copy-start(pred[24,2304]{1,0:T(8,128)(4,1)} %and_and_fusion) | copy-start | bytes 165892
  619.5 17.4 %all-to-all-start.9 = ((bf16[4,2,55296]{2,1,0:T(2,128)(2,1)}), bf16[4,2,55296]{2,1,0:T(2,128)(2,1)}, u32[]{:S(2)}, u32[]{:S(2)}) async-start(bf16[4,2,55296]{2,1,0:T(2,128)(2,1)} %reshape.1369), calls=%async_computation.9 | async-start | bytes 1769472 | tf_op jit(solution)/shard_map/all_to_all | solution.py:123
  645.6 9.0 %copy-start.29 = (bf16[1,4,8,24]{3,2,1,0:T(8,128)(2,1)S(1)}, bf16[1,4,8,24]{3,2,1,0:T(8,128)(2,1)}, u32[]{:S(2)}) copy-start(bf16[1,4,8,24]{3,2,1,0:T(8,128)(2,1)} %copy-done.27) | copy-start | bytes 4612
  645.6 9.0 %copy-start.33 = (bf16[1,4,8,24]{3,2,1,0:T(8,128)(2,1)S(1)}, bf16[1,4,8,24]{3,2,1,0:T(8,128)(2,1)}, u32[]{:S(2)}) copy-start(bf16[1,4,8,24]{3,2,1,0:T(8,128)(2,1)} %copy-done.31) | copy-start | bytes 4612
  714.5 10.2 %copy-start.23 = (bf16[1,8,64,4,96]{4,2,3,1,0:T(8,128)(2,1)S(1)}, bf16[1,8,64,4,96]{4,2,3,1,0:T(8,128)(2,1)}, u32[]{:S(2)}) copy-start(bf16[1,8,64,4,96]{4,2,3,1,0:T(8,128)(2,1)} %get-tuple-element.46) | copy-start | bytes 1179652
  714.5 10.2 %copy-start.26 = (bf16[1,8,64,4,96]{4,2,3,1,0:T(8,128)(2,1)S(1)}, bf16[1,8,64,4,96]{4,2,3,1,0:T(8,128)(2,1)}, u32[]{:S(2)}) copy-start(bf16[1,8,64,4,96]{4,2,3,1,0:T(8,128)(2,1)} %get-tuple-element.47) | copy-start | bytes 1179652
  (18 other events, 36.7 us)
where the time goes:
time: 853 us; the launch traced here: 845 us
  local copies, waits for them, and re-layouts  566 us (66%)
  waiting for transfers between devices  89.2 us (10%)
  blocking collectives  58.6 us (7%)
  starting transfers between devices  46 us (5%)
  matrix products  41.3 us (5%)
  other arithmetic  40.8 us (5%)
    unnamed x100, local copies, waits for them, and re-layouts  187 us
    another operation x9, local copies, waits for them, and re-layouts, pair_sum(): return jnp.stack([real_part, imag_part], axis=stack_axis)  126 us
    all_to_all x3, waiting for transfers between devices, forward(): lax.all_to_all(x_lines, 'col', split_axis=0, concat_axis=2, tiled=True)  60.6 us
    all_to_all x1, blocking collectives, inverse(): lax.all_to_all(spread, 'col', split_axis=2, concat_axis=0, tiled=True)  40.3 us
    all_to_all x3, local copies, waits for them, and re-layouts, inverse(): lax.all_to_all(spread, 'col', split_axis=2, concat_axis=0, tiled=True)  35.3 us
    convert_element_type x3, local copies, waits for them, and re-layouts, back_y(): joined = pair_sum(pieces, 1, 3).astype(jnp.bfloat16)  34.9 us
    reshape x3, local copies, waits for them, and re-layouts, back_x(): shaped = incoming.reshape(KC, field_count, 2, rows_y, planes)  27.1 us
    all_to_all x3, waiting for transfers between devices, forward(): lax.all_to_all(spread, 'row', split_axis=3, concat_axis=3, tiled=True)  25.1 us
  transfers between devices with their start and end apart: 10, of which 7 were waited for; matrix products, arithmetic and copies ran while one was open for 23% of the time, Pallas kernels for 0%

commit v1 on v0

--- a/solution.py
+++ b/solution.py
@@ -2,7 +2,11 @@
 
 import jax
 import jax.numpy as jnp
+import ml_dtypes
+import numpy as np
 from jax import lax
+from jax.experimental import pallas as pl
+from jax.experimental.pallas import tpu as pltpu
 from jax.sharding import PartitionSpec as P
 
 NX = 512
@@ -55,7 +59,7 @@
     )
 
 
-def on_device(phase, velocity):
+def plain_device(phase, velocity):
     col_count = lax.axis_size("col")
     row_count = lax.axis_size("row")
     rows_y = phase.shape[0]
@@ -186,7 +190,320 @@
     return (result[0], result[1:4])
 
 
+def tables(cols, rows, rows_y, planes):
+    total_z = planes * rows
+    half_z = 3 * total_z // 8
+    modes_z = 2 * half_z
+    kx_local = KC // cols
+
+    def pair(first, second, period):
+        residue = first[:, None] * second[None, :] % period
+        angles = residue.astype(np.float32) * np.float32(2.0 * math.pi / period)
+        return [np.cos(angles).astype(ml_dtypes.bfloat16), np.sin(angles).astype(ml_dtypes.bfloat16)]
+
+    cos_x, sin_x = pair(np.arange(KC), np.arange(NX), NX)
+    cos_y, sin_y = pair(np.arange(NY), np.arange(KY) - KC, NY)
+    cos_z, sin_z = pair(np.arange(total_z), np.arange(modes_z) - half_z, total_z)
+    x_forward = np.stack([cos_x, -sin_x]).reshape(2, cols, kx_local, NX)
+    x_forward = x_forward.transpose(1, 0, 2, 3).reshape(2 * KC, NX)
+    weight = np.where(np.arange(KC) == 0, 1.0, 2.0).astype(ml_dtypes.bfloat16)[:, None]
+    x_inverse = np.stack([cos_x * weight, -(sin_x * weight)]).reshape(2, cols, kx_local, NX)
+    x_inverse = x_inverse.transpose(1, 0, 2, 3).reshape(2 * KC, NX)
+    y_forward = np.concatenate([cos_y, sin_y], axis=1)
+    y_inverse = np.concatenate([cos_y.T, sin_y.T], axis=1)
+    cz, sz = (t.reshape(rows, planes, modes_z) for t in (cos_z, sin_z))
+    z_forward = np.stack([np.stack([cz, sz], 1), np.stack([-sz, cz], 1)])
+    z_forward = z_forward.transpose(0, 4, 1, 2, 3).reshape(2 * modes_z, 2 * total_z)
+    z_inverse = np.stack([np.stack([cz, -sz], 2), np.stack([sz, cz], 2)], 1)
+    z_inverse = z_inverse.reshape(2 * total_z, 2 * modes_z)
+    return [jnp.asarray(t.astype(ml_dtypes.bfloat16)) for t in (x_forward, x_inverse, y_forward, y_inverse, z_forward, z_inverse)]
+
+
+def dot(first, second, dims=((1,), (0,))):
+    return lax.dot_general(first, second, (dims, ((), ())), preferred_element_type=jnp.float32)
+
+
+def whole(array):
+    return pl.BlockSpec(array.shape, lambda *_: (0,) * array.ndim)
+
+
+def call(body, grid, in_specs, out_specs, out_shape, flops, moved, scratch=()):
+    return pl.pallas_call(
+        body,
+        grid=grid,
+        in_specs=in_specs,
+        out_specs=out_specs,
+        out_shape=out_shape,
+        scratch_shapes=list(scratch),
+        compiler_params=pltpu.CompilerParams(vmem_limit_bytes=40 * 1024 * 1024),
+        cost_estimate=pl.CostEstimate(flops=flops, bytes_accessed=moved, transcendentals=0),
+    )
+
+
+COST = 400_000_000
+
+
+def fast_device(sizes, phase, velocity):
+    cols, rows, rows_y, planes = sizes
+    total_z = planes * rows
+    half_z = 3 * total_z // 8
+    modes_z = 2 * half_z
+    kx_local = KC // cols
+    a_local = kx_local // rows
+    lanes = a_local * KY
+    points = rows_y * planes
+    scale_inv = 1.0 / (NX * NY * total_z)
+    tx_f, tx_i, ty_f, ty_i, tz_f, tz_i = tables(cols, rows, rows_y, planes)
+    f32, bf16 = jnp.float32, jnp.bfloat16
+
+    def x_forward(fields):
+        count = fields.shape[0]
+
+        def body(field_ref, table_ref, out_ref):
+            lines = jnp.swapaxes(field_ref[0], 0, 1).reshape(points, NX).astype(bf16)
+            made = dot(table_ref[...], lines, ((1,), (1,))).astype(bf16)
+            out_ref[...] = made.reshape(cols, 1, 2 * kx_local, points)
+
+        return call(
+            body,
+            (count,),
+            [pl.BlockSpec((1, rows_y, planes, NX), lambda i: (i, 0, 0, 0)), whole(tx_f)],
+            pl.BlockSpec((cols, 1, 2 * kx_local, points), lambda i: (0, i, 0, 0)),
+            jax.ShapeDtypeStruct((cols, count, 2 * kx_local, points), bf16),
+            COST * count,
+            1 << 20,
+        )(fields, tx_f)
+
+    def y_forward(incoming):
+        count = incoming.shape[1]
+
+        def body(in_ref, table_ref, out_ref):
+            lhs = jnp.concatenate(
+                [
+                    jnp.concatenate(
+                        [in_ref[c, 0, :, z * rows_y : (z + 1) * rows_y] for c in range(cols)], axis=1
+                    )
+                    for z in range(planes)
+                ],
+                axis=0,
+            )
+            made = dot(lhs, table_ref[...]).reshape(planes, 2 * kx_local, 2 * KY)
+            first, second = made[:, :kx_local], made[:, kx_local:]
+            real = jnp.swapaxes(first[:, :, :KY] + second[:, :, KY:], 0, 1)
+            imag = jnp.swapaxes(second[:, :, :KY] - first[:, :, KY:], 0, 1)
+            both = jnp.concatenate([real, imag], axis=1).astype(bf16)
+            for a in range(kx_local):
+                r, k = a // a_local, a % a_local
+                out_ref[r, 0, :, k * KY : (k + 1) * KY] = both[a]
+
+        return call(
+            body,
+            (count,),
+            [pl.BlockSpec((cols, 1, 2 * kx_local, points), lambda i: (0, i, 0, 0)), whole(ty_f)],
+            pl.BlockSpec((rows, 1, 2 * planes, lanes), lambda i: (0, i, 0, 0)),
+            jax.ShapeDtypeStruct((rows, count, 2 * planes, lanes), bf16),
+            COST * count,
+            1 << 20,
+        )(incoming, ty_f)
+
+    def y_inverse(incoming):
+        count = incoming.shape[1]
+
+        def body(in_ref, table_ref, out_ref):
+            lhs = jnp.concatenate(
+                [
+                    in_ref[r, 0, :, k * KY : (k + 1) * KY]
+                    for r in range(rows)
+                    for k in range(a_local)
+                ],
+                axis=0,
+            )
+            made = dot(lhs, table_ref[...]).reshape(kx_local, 2 * planes, 2 * NY)
+            first, second = made[:, :planes], made[:, planes:]
+            real = jnp.swapaxes(first[:, :, :NY] - second[:, :, NY:], 0, 1)
+            imag = jnp.swapaxes(first[:, :, NY:] + second[:, :, :NY], 0, 1)
+            both = jnp.concatenate([real, imag], axis=1).astype(bf16)
+            for c in range(cols):
+                out_ref[c, 0] = jnp.concatenate(
+                    [both[z, :, c * rows_y : (c + 1) * rows_y] for z in range(planes)], axis=1
+                )
+
+        return call(
+            body,
+            (count,),
+            [pl.BlockSpec((rows, 1, 2 * planes, lanes), lambda i: (0, i, 0, 0)), whole(ty_i)],
+            pl.BlockSpec((cols, 1, 2 * kx_local, points), lambda i: (0, i, 0, 0)),
+            jax.ShapeDtypeStruct((cols, count, 2 * kx_local, points), bf16),
+            COST * count,
+            1 << 20,
+        )(incoming, ty_i)
+
+    def x_inverse(incoming):
+        count = incoming.shape[1]
+
+        def body(in_ref, table_ref, out_ref):
+            lines = in_ref[...].reshape(2 * KC, points)
+            made = dot(lines, table_ref[...], ((0,), (0,)))
+            out_ref[0] = jnp.swapaxes(made.reshape(planes, rows_y, NX), 0, 1)
+
+        return call(
+            body,
+            (count,),
+            [pl.BlockSpec((cols, 1, 2 * kx_local, points), lambda i: (0, i, 0, 0)), whole(tx_i)],
+            pl.BlockSpec((1, rows_y, planes, NX), lambda i: (i, 0, 0, 0)),
+            jax.ShapeDtypeStruct((count, rows_y, planes, NX), f32),
+            COST * count,
+            1 << 20,
+        )(incoming, tx_i)
+
+    def over_col(values):
+        return lax.all_to_all(values, "col", split_axis=0, concat_axis=0, tiled=True)
+
+    def over_row(values):
+        return lax.all_to_all(values, "row", split_axis=0, concat_axis=0, tiled=True)
+
+    def forward(fields):
+        return over_row(y_forward(over_col(x_forward(fields))))
+
+    def inverse(outgoing):
+        return x_inverse(over_col(y_inverse(over_row(outgoing))))
+
+    cut = KY
+    steps = lanes // cut
+    first_a = lax.axis_index("col") * kx_local + lax.axis_index("row") * a_local
+    wave_x = first_a.astype(f32) + jnp.repeat(jnp.arange(a_local, dtype=f32), KY)
+    wave_y = jnp.tile(jnp.arange(KY, dtype=f32) - KC, a_local)
+    wave_xy = jnp.stack([wave_x, wave_y])
+
+    def coefficient(in_ref, f, table_ref):
+        stacked = jnp.concatenate([in_ref[r, f] for r in range(rows)], axis=0)
+        return dot(table_ref[...], stacked) * scale_inv
+
+    def emit(out_ref, f, real, imag, table_ref):
+        both = jnp.concatenate([real, imag], axis=0).astype(bf16)
+        made = dot(table_ref[...], both).astype(bf16)
+        for r in range(rows):
+            out_ref[r, f] = made[r * 2 * planes : (r + 1) * 2 * planes]
+
+    def waves(wave_ref):
+        wx, wy = wave_ref[0:1, :], wave_ref[1:2, :]
+        m = lax.broadcasted_iota(jnp.int32, (modes_z, cut), 0) - half_z
+        wz = m.astype(f32) * (NX / total_z)
+        return wx, wy, wz, wx * wx + wy * wy + wz * wz
+
+    def lines_spec(count):
+        return pl.BlockSpec((rows, count, 2 * planes, cut), lambda i: (0, 0, 0, i))
+
+    def coeff_spec(count):
+        return pl.BlockSpec((count, 2 * modes_z, cut), lambda i: (0, 0, i))
+
+    def lines_shape(count):
+        return jax.ShapeDtypeStruct((rows, count, 2 * planes, lanes), bf16)
+
+    def coeff_shape(count):
+        return jax.ShapeDtypeStruct((count, 2 * modes_z, lanes), f32)
+
+    wave_spec = pl.BlockSpec((2, cut), lambda i: (0, i))
+
+    def phase_spectral(in_ref, wave_ref, f_ref, i_ref, coeff_ref, out_ref):
+        wx, wy, wz, k2 = waves(wave_ref)
+        c = coefficient(in_ref, 0, f_ref)
+        coeff_ref[0] = c
+        re, im = c[:modes_z], c[modes_z:]
+        emit(out_ref, 0, -(wx * im), wx * re, i_ref)
+        emit(out_ref, 1, -(wy * im), wy * re, i_ref)
+        emit(out_ref, 2, -(wz * im), wz * re, i_ref)
+        emit(out_ref, 3, -k2 * re, -k2 * im, i_ref)
+
+    def flow_spectral(in_ref, wave_ref, f_ref, i_ref, coeff_ref, out_ref):
+        wx, wy, wz, _ = waves(wave_ref)
+        cs = [coefficient(in_ref, j, f_ref) for j in range(3)]
+        for j in range(3):
+            coeff_ref[j] = cs[j]
+        re, im = [c[:modes_z] for c in cs], [c[modes_z:] for c in cs]
+        w = [wx, wy, wz]
+        for j in range(3):
+            p, q = (j + 1) % 3, (j + 2) % 3
+            emit(
+                out_ref,
+                j,
+                -(w[p] * im[q] - w[q] * im[p]),
+                w[p] * re[q] - w[q] * re[p],
+                i_ref,
+            )
+
+    def phase_solve(adv_ref, bulk_ref, old_ref, wave_ref, f_ref, i_ref, out_ref):
+        wx, wy, wz, k2 = waves(wave_ref)
+        adv = coefficient(adv_ref, 0, f_ref)
+        bulk = coefficient(bulk_ref, 0, f_ref)
+        old = old_ref[0]
+        mean_mode = (wx == 0) & (wy == 0) & (wz == 0)
+        stable = 1.0 / time_step + mobility * stabilizer * k2
+        below = stable + mobility * epsilon * epsilon * k2 * k2
+        parts = []
+        for p in range(2):
+            at = slice(p * modes_z, (p + 1) * modes_z)
+            kept = jnp.where(mean_mode, 0.0, adv[at])
+            parts.append((stable * old[at] - kept - mobility * k2 * bulk[at]) / below)
+        emit(out_ref, 0, parts[0], parts[1], i_ref)
+
+    def flow_solve(force_ref, old_ref, wave_ref, f_ref, i_ref, out_ref):
+        wx, wy, wz, k2 = waves(wave_ref)
+        viscous = 1.0 / time_step + k2 / reynolds
+        largest = jnp.maximum(k2, 1.0)
+        w = [wx, wy, wz]
+        force = [coefficient(force_ref, j, f_ref) for j in range(3)]
+        made = [[], [], []]
+        for p in range(2):
+            at = slice(p * modes_z, (p + 1) * modes_z)
+            free = [(old_ref[j, at] / time_step + force[j][at]) / viscous for j in range(3)]
+            normal = (wx * free[0] + wy * free[1] + wz * free[2]) / largest
+            for j in range(3):
+                made[j].append(free[j] - w[j] * normal)
+        for j in range(3):
+            emit(out_ref, j, made[j][0], made[j][1], i_ref)
+
+    phase_lines = forward(phase[None])
+    flow_lines = forward(velocity)
+    bulk_field = phase * phase * phase - phase
+    bulk_lines = forward(bulk_field[None])
+    tail = [wave_spec, whole(tz_f), whole(tz_i)]
+    last = (wave_xy, tz_f, tz_i)
+    coeff_phase, gradient_lines = call(
+        phase_spectral, (steps,), [lines_spec(1)] + tail,
+        [coeff_spec(1), lines_spec(4)], [coeff_shape(1), lines_shape(4)], COST, 1 << 20,
+    )(phase_lines, *last)
+    coeff_flow, vortex_lines = call(
+        flow_spectral, (steps,), [lines_spec(3)] + tail,
+        [coeff_spec(3), lines_spec(3)], [coeff_shape(3), lines_shape(3)], COST, 1 << 20,
+    )(flow_lines, *last)
+    leading = inverse(gradient_lines)
+    vortex = inverse(vortex_lines)
+    advect, _, potential = phase_terms(phase, velocity, leading[0:3], leading[3])
+    advect_lines = forward(advect[None])
+    force_lines = forward(momentum(velocity, vortex, leading[0:3], potential))
+    new_phase = call(
+        phase_solve, (steps,), [lines_spec(1), lines_spec(1), coeff_spec(1)] + tail,
+        lines_spec(1), lines_shape(1), COST, 1 << 20,
+    )(advect_lines, bulk_lines, coeff_phase, *last)
+    new_flow = call(
+        flow_solve, (steps,), [lines_spec(3), coeff_spec(3)] + tail,
+        lines_spec(3), lines_shape(3), COST, 1 << 20,
+    )(force_lines, coeff_flow, *last)
+    return (inverse(new_phase)[0], inverse(new_flow))
+
+
 def solution(mesh):
+    cols, rows = mesh.shape["col"], mesh.shape["row"]
+
+    def on_device(phase, velocity):
+        rows_y, planes = phase.shape[0], phase.shape[1]
+        kx_local = KC // cols
+        aligned = planes % 8 == 0 and kx_local % (8 * rows // math.gcd(8, rows)) == 0
+        if aligned and (rows_y * planes) % 128 == 0:
+            return fast_device((cols, rows, rows_y, planes), phase, velocity)
+        return plain_device(phase, velocity)
+
     return jax.shard_map(
         on_device,
         mesh=mesh,

time: 853 us -> 384 us (0.45)
  local copies, waits for them, and re-layouts: 566 us -> 39.4 us
  waiting for transfers between devices: 89.2 us -> 190 us
  Pallas kernels: 0 us -> 56.4 us
  matrix products: 41.3 us -> 0 us
  blocking collectives: 58.6 us -> 19.1 us
  other arithmetic: 40.8 us -> 7.59 us
  starting transfers between devices: 46 us -> 67.3 us
    another operation x49 -> x0, local copies, waits for them, and re-layouts: 173 us -> none  [the longest x9 126 us: pair_sum(): return jnp.stack([real_part, imag_part], axis=stack_axis)]
    unnamed x100 -> x95, local copies, waits for them, and re-layouts: 187 us -> 39.4 us
    all_to_all x10 -> x17, waiting for transfers between devices: 89.2 us -> 190 us  [the longest x8 146 us: over_col(): lax.all_to_all(values, 'col', split_axis=0, concat_axis=0, tiled=True)]
    reshape x11 -> x0, local copies, waits for them, and re-layouts: 71.8 us -> none  [the longest x3 27.1 us: back_x(): shaped = incoming.reshape(KC, field_count, 2, rows_y, planes)]
    pallas_call x0 -> x22, Pallas kernels: none -> 56.4 us  [the longest x4 12.7 us: x_inverse(): call(body, (count,), [pl.BlockSpec((cols, 1, 2 * kx_local, points), lambd...]
    all_to_all x9 -> x0, local copies, waits for them, and re-layouts: 51.4 us -> none  [the longest x3 35.3 us: inverse(): lax.all_to_all(spread, 'col', split_axis=2, concat_axis=0, tiled=True)]
    convert_element_type x6 -> x0, local copies, waits for them, and re-layouts: 41.6 us -> none  [the longest x3 34.9 us: back_y(): joined = pair_sum(pieces, 1, 3).astype(jnp.bfloat16)]
    dot_general x18 -> x0, matrix products: 41.3 us -> none  [the longest x3 19.6 us: back_y(): jnp.einsum('afprzb,tcyrb->ptafcyz', shaped, y_inverse, preferred_element_...]
  transfers between devices with their start and end apart: 10 -> 17, of which waited for: 7 -> 16; matrix products, arithmetic and copies ran while one was open for 23% -> 2% of each run, Pallas kernels for 0% -> 14%
where the time goes in v1:
time: 384 us; the launch traced here: 381 us
  waiting for transfers between devices  190 us (49%)
  starting transfers between devices  67.3 us (18%)
  Pallas kernels  56.4 us (15%)
  local copies, waits for them, and re-layouts  39.4 us (10%)
  blocking collectives  19.1 us (5%)
  other arithmetic  7.59 us (2%)
    all_to_all x8, waiting for transfers between devices, over_col(): lax.all_to_all(values, 'col', split_axis=0, concat_axis=0, tiled=True)  146 us
    all_to_all x9, waiting for transfers between devices, over_row(): lax.all_to_all(values, 'row', split_axis=0, concat_axis=0, tiled=True)  43.7 us
    unnamed x95, local copies, waits for them, and re-layouts  39.4 us
    all_to_all x9, starting transfers between devices, over_row(): lax.all_to_all(values, 'row', split_axis=0, concat_axis=0, tiled=True)  34.8 us
    all_to_all x8, starting transfers between devices, over_col(): lax.all_to_all(values, 'col', split_axis=0, concat_axis=0, tiled=True)  32.5 us
    all_to_all x1, blocking collectives, over_col(): lax.all_to_all(values, 'col', split_axis=0, concat_axis=0, tiled=True)  19.1 us
    pallas_call x4, Pallas kernels, x_inverse(): call(body, (count,), [pl.BlockSpec((cols, 1, 2 * kx_local, points), lambd...  12.7 us
    pallas_call x4, Pallas kernels, y_inverse(): call(body, (count,), [pl.BlockSpec((rows, 1, 2 * planes, lanes), lambda i...  11.7 us
  transfers between devices with their start and end apart: 17, of which 16 were waited for; matrix products, arithmetic and copies ran while one was open for 2% of the time, Pallas kernels for 14%

profile of v1, /device:TPU:0, one launch (start us, length us, event | category | flops | bytes accessed | tf_op | source)
XLA Modules:
  0.0 381.1 jit_solution(14432588529888580479)
XLA Ops:
  3.5 19.1 %all_to_all.90.in_ref = bf16[8,1,48,512]{3,2,1,0:T(8,128)(2,1)S(1)} all-to-all(bf16[8,1,48,512]{3,2,1,0:T(8,128)(2,1)S(1)} %shard_map.95), channel_id=1, replica_groups=mesh['row'=4,'col'=8] {'col'}, dimensions={0} | all-to-all | bytes 786432 | tf_op jit(solution)/shard_map/all_to_all | solution.py:360
  25.1 4.1 %all-to-all-start.1 = ((bf16[4,1,16,2304]{3,2,1,0:T(8,128)(2,1)}), bf16[4,1,16,2304]{3,2,1,0:T(8,128)(2,1)}, u32[]{:S(2)}, u32[]{:S(2)}) async-start(bf16[4,1,16,2304]{3,2,1,0:T(8,128)(2,1)} %copy-done.27), calls=%async_computation.1 | async-start | bytes 589824 | tf_op jit(solution)/shard_map/all_to_all | solution.py:363
  31.8 3.8 %all-to-all-done.1.in_ref = bf16[4,1,16,2304]{3,2,1,0:T(8,128)(2,1)} async-done(((bf16[4,1,16,2304]{3,2,1,0:T(8,128)(2,1)}), bf16[4,1,16,2304]{3,2,1,0:T(8,128)(2,1)}, u32[]{:S(2)}, u32[]{:S(2)}) %all-to-all-start.1) | async-done | bytes 294944 | tf_op jit(solution)/shard_map/all_to_all | solution.py:363
  35.6 4.3 %all-to-all-start.10 = ((bf16[8,3,48,512]{3,2,1,0:T(8,128)(2,1)}), bf16[8,3,48,512]{3,2,1,0:T(8,128)(2,1)}, u32[]{:S(2)}, u32[]{:S(2)}) async-start(bf16[8,3,48,512]{3,2,1,0:T(8,128)(2,1)} %copy-done.8), calls=%async_computation.10 | async-start | bytes 2359296 | tf_op jit(solution)/shard_map/all_to_all | solution.py:360
  40.7 3.8 %shard_map.97 = (f32[1,48,2304]{2,1,0:T(8,128)S(1)}, bf16[4,4,16,2304]{3,2,1,0:T(8,128)(2,1)S(1)}) custom-call(bf16[4,1,16,2304]{3,2,1,0:T(8,128)(2,1)} %all-to-all-done.1.in_ref, f32[2,2304]{1,0:T(2,128)S(1)} %pad_maximum_fusion.1.wave_ref, bf16[48,64]{1,0:T(8,128)(2,1)S(1)} %copy-done.32, bf16[64,48]{1,0:T(8,128)(2,1)S(1)} %copy-done.31), custom_call_target="tpu_custom_call" | custom-call | flops 400000000 | bytes 1048576 | tf_op jit(solution)/shard_map/pallas_call | solution.py:472
  47.0 21.4 %all-to-all-done.10.in_ref = bf16[8,3,48,512]{3,2,1,0:T(8,128)(2,1)} async-done(((bf16[8,3,48,512]{3,2,1,0:T(8,128)(2,1)}), bf16[8,3,48,512]{3,2,1,0:T(8,128)(2,1)}, u32[]{:S(2)}, u32[]{:S(2)}) %all-to-all-start.10) | async-done | bytes 1179680 | tf_op jit(solution)/shard_map/all_to_all | solution.py:360
  68.4 4.3 %all-to-all-start.2 = ((bf16[4,4,16,2304]{3,2,1,0:T(8,128)(2,1)}), bf16[4,4,16,2304]{3,2,1,0:T(8,128)(2,1)}, u32[]{:S(2)}, u32[]{:S(2)}) async-start(bf16[4,4,16,2304]{3,2,1,0:T(8,128)(2,1)} %copy-done.19), calls=%async_computation.2 | async-start | bytes 2359296 | tf_op jit(solution)/shard_map/all_to_all | solution.py:363
  78.0 10.6 %all-to-all-done.2.in_ref = bf16[4,4,16,2304]{3,2,1,0:T(8,128)(2,1)} async-done(((bf16[4,4,16,2304]{3,2,1,0:T(8,128)(2,1)}), bf16[4,4,16,2304]{3,2,1,0:T(8,128)(2,1)}, u32[]{:S(2)}, u32[]{:S(2)}) %all-to-all-start.2) | async-done | bytes 1179680 | tf_op jit(solution)/shard_map/all_to_all | solution.py:363
  88.6 4.2 %all-to-all-start.11 = ((bf16[4,3,16,2304]{3,2,1,0:T(8,128)(2,1)}), bf16[4,3,16,2304]{3,2,1,0:T(8,128)(2,1)}, u32[]{:S(2)}, u32[]{:S(2)}) async-start(bf16[4,3,16,2304]{3,2,1,0:T(8,128)(2,1)} %copy-done.25), calls=%async_computation.11 | async-start | bytes 1769472 | tf_op jit(solution)/shard_map/all_to_all | solution.py:363
  94.0 4.3 %shard_map.98 = bf16[8,4,48,512]{3,2,1,0:T(8,128)(2,1)S(1)} custom-call(bf16[4,4,16,2304]{3,2,1,0:T(8,128)(2,1)} %all-to-all-done.2.in_ref, bf16[384,1024]{1,0:T(8,128)(2,1)S(1)} %copy-done.35), custom_call_target="tpu_custom_call" | custom-call | flops 1600000000 | bytes 1048576 | tf_op jit(solution)/shard_map/pallas_call | solution.py:331
  99.4 6.1 %all-to-all-done.11.in_ref = bf16[4,3,16,2304]{3,2,1,0:T(8,128)(2,1)} async-done(((bf16[4,3,16,2304]{3,2,1,0:T(8,128)(2,1)}), bf16[4,3,16,2304]{3,2,1,0:T(8,128)(2,1)}, u32[]{:S(2)}, u32[]{:S(2)}) %all-to-all-start.11) | async-done | bytes 884768 | tf_op jit(solution)/shard_map/all_to_all | solution.py:363
  105.6 4.3 %all-to-all-start.3 = ((bf16[8,4,48,512]{3,2,1,0:T(8,128)(2,1)}), bf16[8,4,48,512]{3,2,1,0:T(8,128)(2,1)}, u32[]{:S(2)}, u32[]{:S(2)}) async-start(bf16[8,4,48,512]{3,2,1,0:T(8,128)(2,1)} %copy-done.13), calls=%async_computation.3 | async-start | bytes 3145728 | tf_op jit(solution)/shard_map/all_to_all | solution.py:360
  111.3 4.3 %shard_map.109 = (f32[3,48,2304]{2,1,0:T(8,128)S(1)}, bf16[4,3,16,2304]{3,2,1,0:T(8,128)(2,1)S(1)}) custom-call(bf16[4,3,16,2304]{3,2,1,0:T(8,128)(2,1)} %all-to-all-done.11.in_ref, f32[2,2304]{1,0:T(2,128)S(1)} %copy-done.29, bf16[48,64]{1,0:T(8,128)(2,1)S(1)} %copy-done.33, bf16[64,48]{1,0:T(8,128)(2,1)S(1)} %copy-done.31), custom_call_target="tpu_custom_call" | custom-call | flops 400000000 | bytes 1048576 | tf_op jit(solution)/shard_map/pallas_call | solution.py:476
  117.6 29.2 %all-to-all-done.3.in_ref = bf16[8,4,48,512]{3,2,1,0:T(8,128)(2,1)} async-done(((bf16[8,4,48,512]{3,2,1,0:T(8,128)(2,1)}), bf16[8,4,48,512]{3,2,1,0:T(8,128)(2,1)}, u32[]{:S(2)}, u32[]{:S(2)}) %all-to-all-start.3) | async-done | bytes 1572896 | tf_op jit(solution)/shard_map/all_to_all | solution.py:360
  146.9 4.2 %all-to-all-start.12 = ((bf16[4,3,16,2304]{3,2,1,0:T(8,128)(2,1)}), bf16[4,3,16,2304]{3,2,1,0:T(8,128)(2,1)}, u32[]{:S(2)}, u32[]{:S(2)}) async-start(bf16[4,3,16,2304]{3,2,1,0:T(8,128)(2,1)} %copy-done.22), calls=%async_computation.12 | async-start | bytes 1769472 | tf_op jit(solution)/shard_map/all_to_all | solution.py:363
  152.1 3.8 shard_map.99
  159.2 4.7 %all-to-all-done.12.in_ref = bf16[4,3,16,2304]{3,2,1,0:T(8,128)(2,1)} async-done(((bf16[4,3,16,2304]{3,2,1,0:T(8,128)(2,1)}), bf16[4,3,16,2304]{3,2,1,0:T(8,128)(2,1)}, u32[]{:S(2)}, u32[]{:S(2)}) %all-to-all-start.12) | async-done | bytes 884768 | tf_op jit(solution)/shard_map/all_to_all | solution.py:363
  163.8 4.1 %all-to-all-start.4 = ((bf16[8,1,48,512]{3,2,1,0:T(8,128)(2,1)}), bf16[8,1,48,512]{3,2,1,0:T(8,128)(2,1)}, u32[]{:S(2)}, u32[]{:S(2)}) async-start(bf16[8,1,48,512]{3,2,1,0:T(8,128)(2,1)} %copy-done.14), calls=%async_computation.4 | async-start | bytes 786432 | tf_op jit(solution)/shard_map/all_to_all | solution.py:360
  173.6 6.0 %all-to-all-done.4.in_ref = bf16[8,1,48,512]{3,2,1,0:T(8,128)(2,1)} async-done(((bf16[8,1,48,512]{3,2,1,0:T(8,128)(2,1)}), bf16[8,1,48,512]{3,2,1,0:T(8,128)(2,1)}, u32[]{:S(2)}, u32[]{:S(2)}) %all-to-all-start.4) | async-done | bytes 393248 | tf_op jit(solution)/shard_map/all_to_all | solution.py:360
  179.6 4.3 %all-to-all-start.13 = ((bf16[8,3,48,512]{3,2,1,0:T(8,128)(2,1)}), bf16[8,3,48,512]{3,2,1,0:T(8,128)(2,1)}, u32[]{:S(2)}, u32[]{:S(2)}) async-start(bf16[8,3,48,512]{3,2,1,0:T(8,128)(2,1)} %copy-done.21), calls=%async_computation.13 | async-start | bytes 2359296 | tf_op jit(solution)/shard_map/all_to_all | solution.py:360
  187.3 24.7 %all-to-all-done.13.in_ref = bf16[8,3,48,512]{3,2,1,0:T(8,128)(2,1)} async-done(((bf16[8,3,48,512]{3,2,1,0:T(8,128)(2,1)}), bf16[8,3,48,512]{3,2,1,0:T(8,128)(2,1)}, u32[]{:S(2)}, u32[]{:S(2)}) %all-to-all-start.13) | async-done | bytes 1179680 | tf_op jit(solution)/shard_map/all_to_all | solution.py:360
  212.0 4.1 %all-to-all-start.5 = ((bf16[4,1,16,2304]{3,2,1,0:T(8,128)(2,1)}), bf16[4,1,16,2304]{3,2,1,0:T(8,128)(2,1)}, u32[]{:S(2)}, u32[]{:S(2)}) async-start(bf16[4,1,16,2304]{3,2,1,0:T(8,128)(2,1)} %copy-done.26), calls=%async_computation.5 | async-start | bytes 589824 | tf_op jit(solution)/shard_map/all_to_all | solution.py:363
  220.5 4.6 %fusion.7 = (f32[1,64,8,512]{3,2,1,0:T(8,128)}, f32[1,64,8,512]{3,2,1,0:T(8,128)}, f32[1,64,8,512]{3,2,1,0:T(8,128)}, f32[1,64,8,512]{3,2,1,0:T(8,128)S(1)}) fusion(f32[3,64,8,512]{3,2,1,0:T(8,128)S(1)} %shard_map.111, f32[4,64,8,512]{3,2,1,0:T(8,128)S(1)} %copy-done.1, f32[3,64,8,512]{3,2,1,0:T(8,128)S(1)} %copy-done.2, f32[64,8,512]{2,1,0:T(8,128)} %param.8), kind=kLoop, calls=%fused_computation.13 | loop fusion | flops 5242880 | bytes 15728640 | tf_op jit(solution)/shard_map/stack | solution.py:53
  226.3 4.1 %all-to-all-start.6 = ((bf16[8,1,48,512]{3,2,1,0:T(8,128)(2,1)}), bf16[8,1,48,512]{3,2,1,0:T(8,128)(2,1)}, u32[]{:S(2)}, u32[]{:S(2)}) async-start(bf16[8,1,48,512]{3,2,1,0:T(8,128)(2,1)} %shard_map.102), calls=%async_computation.6 | async-start | bytes 786432 | tf_op jit(solution)/shard_map/all_to_all | solution.py:360
  235.1 7.9 %all-to-all-done.6.in_ref = bf16[8,1,48,512]{3,2,1,0:T(8,128)(2,1)} async-done(((bf16[8,1,48,512]{3,2,1,0:T(8,128)(2,1)}), bf16[8,1,48,512]{3,2,1,0:T(8,128)(2,1)}, u32[]{:S(2)}, u32[]{:S(2)}) %all-to-all-start.6) | async-done | bytes 393248 | tf_op jit(solution)/shard_map/all_to_all | solution.py:360
  250.2 25.3 %all-to-all-done.14.in_ref = bf16[8,3,48,512]{3,2,1,0:T(8,128)(2,1)S(1)} async-done(((bf16[8,3,48,512]{3,2,1,0:T(8,128)(2,1)}), bf16[8,3,48,512]{3,2,1,0:T(8,128)(2,1)S(1)}, u32[]{:S(2)}, u32[]{:S(2)}) %all-to-all-start.14) | async-done | bytes 1179680 | tf_op jit(solution)/shard_map/all_to_all | solution.py:360
  290.8 4.6 %shard_map.104 = bf16[4,1,16,2304]{3,2,1,0:T(8,128)(2,1)} custom-call(bf16[4,1,16,2304]{3,2,1,0:T(8,128)(2,1)} %all-to-all-done.5.adv_ref, bf16[4,1,16,2304]{3,2,1,0:T(8,128)(2,1)S(1)} %all-to-all-done.7.bulk_ref, f32[1,48,2304]{2,1,0:T(8,128)S(1)} %copy-done.45, f32[2,2304]{1,0:T(2,128)S(1)} %copy-done.30, bf16[48,64]{1,0:T(8,128)(2,1)S(1)} %copy-done.34, ...), custom_call_target="tpu_custom_call" | custom-call | flops 400000000 | bytes 1048576 | tf_op jit(solution)/shard_map/pallas_call | solution.py:485
  295.4 7.0 %all-to-all-done.15.force_ref = bf16[4,3,16,2304]{3,2,1,0:T(8,128)(2,1)S(1)} async-done(((bf16[4,3,16,2304]{3,2,1,0:T(8,128)(2,1)}), bf16[4,3,16,2304]{3,2,1,0:T(8,128)(2,1)S(1)}, u32[]{:S(2)}, u32[]{:S(2)}) %all-to-all-start.15) | async-done | bytes 884768 | tf_op jit(solution)/shard_map/all_to_all | solution.py:363
  319.2 10.0 %all-to-all-done.16.in_ref = bf16[4,3,16,2304]{3,2,1,0:T(8,128)(2,1)S(1)} async-done(((bf16[4,3,16,2304]{3,2,1,0:T(8,128)(2,1)}), bf16[4,3,16,2304]{3,2,1,0:T(8,128)(2,1)S(1)}, u32[]{:S(2)}, u32[]{:S(2)}) %all-to-all-start.16) | async-done | bytes 884768 | tf_op jit(solution)/shard_map/all_to_all | solution.py:363
  330.1 4.1 %all-to-all-start.9 = ((bf16[8,1,48,512]{3,2,1,0:T(8,128)(2,1)}), bf16[8,1,48,512]{3,2,1,0:T(8,128)(2,1)}, u32[]{:S(2)}, u32[]{:S(2)}) async-start(bf16[8,1,48,512]{3,2,1,0:T(8,128)(2,1)} %shard_map.105), calls=%async_computation.9 | async-start | bytes 786432 | tf_op jit(solution)/shard_map/all_to_all | solution.py:360
  340.0 5.9 %all-to-all-done.9.in_ref = bf16[8,1,48,512]{3,2,1,0:T(8,128)(2,1)} async-done(((bf16[8,1,48,512]{3,2,1,0:T(8,128)(2,1)}), bf16[8,1,48,512]{3,2,1,0:T(8,128)(2,1)}, u32[]{:S(2)}, u32[]{:S(2)}) %all-to-all-start.9) | async-done | bytes 393248 | tf_op jit(solution)/shard_map/all_to_all | solution.py:360
  352.1 25.9 %all-to-all-done.17.in_ref = bf16[8,3,48,512]{3,2,1,0:T(8,128)(2,1)S(1)} async-done(((bf16[8,3,48,512]{3,2,1,0:T(8,128)(2,1)}), bf16[8,3,48,512]{3,2,1,0:T(8,128)(2,1)S(1)}, u32[]{:S(2)}, u32[]{:S(2)}) %all-to-all-start.17) | async-done | bytes 1179680 | tf_op jit(solution)/shard_map/all_to_all | solution.py:360
  (126 shorter events, 100.8 us)
Async XLA Ops:
  0.6 28.6 %copy-start.2 = (f32[3,64,8,512]{3,2,1,0:T(8,128)S(1)}, f32[3,64,8,512]{3,2,1,0:T(8,128)}, u32[]{:S(2)}) copy-start(f32[3,64,8,512]{3,2,1,0:T(8,128)} %field_ref.1) | copy-start | bytes 9437188
  0.6 1.1 copy-start.3
  1.8 1.2 copy-start.10
  3.0 26.2 %copy-start.4 = (bf16[384,512]{1,0:T(8,128)(2,1)S(1)}, bf16[384,512]{1,0:T(8,128)(2,1)}, u32[]{:S(2)}) copy-start(bf16[384,512]{1,0:T(8,128)(2,1)} %constant.29.clone.table_ref) | copy-start | bytes 1179652
  25.1 10.5 %all-to-all-start.1 = ((bf16[4,1,16,2304]{3,2,1,0:T(8,128)(2,1)}), bf16[4,1,16,2304]{3,2,1,0:T(8,128)(2,1)}, u32[]{:S(2)}, u32[]{:S(2)}) async-start(bf16[4,1,16,2304]{3,2,1,0:T(8,128)(2,1)} %copy-done.27), calls=%async_computation.1 | async-start | bytes 589824 | tf_op jit(solution)/shard_map/all_to_all | solution.py:363
  29.2 10.8 %copy-start.31 = (bf16[64,48]{1,0:T(8,128)(2,1)S(1)}, bf16[64,48]{1,0:T(8,128)(2,1)}, u32[]{:S(2)}) copy-start(bf16[64,48]{1,0:T(8,128)(2,1)} %constant.34.clone.i_ref) | copy-start | bytes 18436
  35.6 32.8 %all-to-all-start.10 = ((bf16[8,3,48,512]{3,2,1,0:T(8,128)(2,1)}), bf16[8,3,48,512]{3,2,1,0:T(8,128)(2,1)}, u32[]{:S(2)}, u32[]{:S(2)}) async-start(bf16[8,3,48,512]{3,2,1,0:T(8,128)(2,1)} %copy-done.8), calls=%async_computation.10 | async-start | bytes 2359296 | tf_op jit(solution)/shard_map/all_to_all | solution.py:360
  68.4 20.2 %all-to-all-start.2 = ((bf16[4,4,16,2304]{3,2,1,0:T(8,128)(2,1)}), bf16[4,4,16,2304]{3,2,1,0:T(8,128)(2,1)}, u32[]{:S(2)}, u32[]{:S(2)}) async-start(bf16[4,4,16,2304]{3,2,1,0:T(8,128)(2,1)} %copy-done.19), calls=%async_computation.2 | async-start | bytes 2359296 | tf_op jit(solution)/shard_map/all_to_all | solution.py:363
  88.6 17.0 %all-to-all-start.11 = ((bf16[4,3,16,2304]{3,2,1,0:T(8,128)(2,1)}), bf16[4,3,16,2304]{3,2,1,0:T(8,128)(2,1)}, u32[]{:S(2)}, u32[]{:S(2)}) async-start(bf16[4,3,16,2304]{3,2,1,0:T(8,128)(2,1)} %copy-done.25), calls=%async_computation.11 | async-start | bytes 1769472 | tf_op jit(solution)/shard_map/all_to_all | solution.py:363
  98.3 1.1 copy-start.13
  105.6 41.3 %all-to-all-start.3 = ((bf16[8,4,48,512]{3,2,1,0:T(8,128)(2,1)}), bf16[8,4,48,512]{3,2,1,0:T(8,128)(2,1)}, u32[]{:S(2)}, u32[]{:S(2)}) async-start(bf16[8,4,48,512]{3,2,1,0:T(8,128)(2,1)} %copy-done.13), calls=%async_computation.3 | async-start | bytes 3145728 | tf_op jit(solution)/shard_map/all_to_all | solution.py:360
  146.9 17.0 %all-to-all-start.12 = ((bf16[4,3,16,2304]{3,2,1,0:T(8,128)(2,1)}), bf16[4,3,16,2304]{3,2,1,0:T(8,128)(2,1)}, u32[]{:S(2)}, u32[]{:S(2)}) async-start(bf16[4,3,16,2304]{3,2,1,0:T(8,128)(2,1)} %copy-done.22), calls=%async_computation.12 | async-start | bytes 1769472 | tf_op jit(solution)/shard_map/all_to_all | solution.py:363
  155.9 2.0 copy-start
  163.8 15.8 %all-to-all-start.4 = ((bf16[8,1,48,512]{3,2,1,0:T(8,128)(2,1)}), bf16[8,1,48,512]{3,2,1,0:T(8,128)(2,1)}, u32[]{:S(2)}, u32[]{:S(2)}) async-start(bf16[8,1,48,512]{3,2,1,0:T(8,128)(2,1)} %copy-done.14), calls=%async_computation.4 | async-start | bytes 786432 | tf_op jit(solution)/shard_map/all_to_all | solution.py:360
  179.6 32.4 %all-to-all-start.13 = ((bf16[8,3,48,512]{3,2,1,0:T(8,128)(2,1)}), bf16[8,3,48,512]{3,2,1,0:T(8,128)(2,1)}, u32[]{:S(2)}, u32[]{:S(2)}) async-start(bf16[8,3,48,512]{3,2,1,0:T(8,128)(2,1)} %copy-done.21), calls=%async_computation.13 | async-start | bytes 2359296 | tf_op jit(solution)/shard_map/all_to_all | solution.py:360
  212.0 14.3 %all-to-all-start.5 = ((bf16[4,1,16,2304]{3,2,1,0:T(8,128)(2,1)}), bf16[4,1,16,2304]{3,2,1,0:T(8,128)(2,1)}, u32[]{:S(2)}, u32[]{:S(2)}) async-start(bf16[4,1,16,2304]{3,2,1,0:T(8,128)(2,1)} %copy-done.26), calls=%async_computation.5 | async-start | bytes 589824 | tf_op jit(solution)/shard_map/all_to_all | solution.py:363
  217.1 3.3 copy-start.1
  226.3 16.7 %all-to-all-start.6 = ((bf16[8,1,48,512]{3,2,1,0:T(8,128)(2,1)}), bf16[8,1,48,512]{3,2,1,0:T(8,128)(2,1)}, u32[]{:S(2)}, u32[]{:S(2)}) async-start(bf16[8,1,48,512]{3,2,1,0:T(8,128)(2,1)} %shard_map.102), calls=%async_computation.6 | async-start | bytes 786432 | tf_op jit(solution)/shard_map/all_to_all | solution.py:360
  243.0 32.5 %all-to-all-start.14 = ((bf16[8,3,48,512]{3,2,1,0:T(8,128)(2,1)}), bf16[8,3,48,512]{3,2,1,0:T(8,128)(2,1)S(1)}, u32[]{:S(2)}, u32[]{:S(2)}) async-start(bf16[8,3,48,512]{3,2,1,0:T(8,128)(2,1)} %copy-done.9), calls=%async_computation.14 | async-start | bytes 2359296 | tf_op jit(solution)/shard_map/all_to_all | solution.py:360
  276.4 9.8 %all-to-all-start.7 = ((bf16[4,1,16,2304]{3,2,1,0:T(8,128)(2,1)}), bf16[4,1,16,2304]{3,2,1,0:T(8,128)(2,1)S(1)}, u32[]{:S(2)}, u32[]{:S(2)}) async-start(bf16[4,1,16,2304]{3,2,1,0:T(8,128)(2,1)} %shard_map.103), calls=%async_computation.7 | async-start | bytes 589824 | tf_op jit(solution)/shard_map/all_to_all | solution.py:363
  279.9 1.3 copy-start.18
  282.3 7.4 %copy-start.30 = (f32[2,2304]{1,0:T(2,128)S(1)}, f32[2,2304]{1,0:T(2,128)}, u32[]{:S(2)}) copy-start(f32[2,2304]{1,0:T(2,128)} %copy-done.28) | copy-start | bytes 55300
  282.3 7.4 %copy-start.34 = (bf16[48,64]{1,0:T(8,128)(2,1)S(1)}, bf16[48,64]{1,0:T(8,128)(2,1)}, u32[]{:S(2)}) copy-start(bf16[48,64]{1,0:T(8,128)(2,1)} %constant.33.clone.f_ref) | copy-start | bytes 18436
  286.2 16.2 %all-to-all-start.15 = ((bf16[4,3,16,2304]{3,2,1,0:T(8,128)(2,1)}), bf16[4,3,16,2304]{3,2,1,0:T(8,128)(2,1)S(1)}, u32[]{:S(2)}, u32[]{:S(2)}) async-start(bf16[4,3,16,2304]{3,2,1,0:T(8,128)(2,1)} %shard_map.113), calls=%async_computation.15 | async-start | bytes 1769472 | tf_op jit(solution)/shard_map/all_to_all | solution.py:363
  303.3 9.8 %all-to-all-start.8 = ((bf16[4,1,16,2304]{3,2,1,0:T(8,128)(2,1)}), bf16[4,1,16,2304]{3,2,1,0:T(8,128)(2,1)S(1)}, u32[]{:S(2)}, u32[]{:S(2)}) async-start(bf16[4,1,16,2304]{3,2,1,0:T(8,128)(2,1)} %shard_map.104), calls=%async_computation.8 | async-start | bytes 589824 | tf_op jit(solution)/shard_map/all_to_all | solution.py:363
  306.8 1.2 copy-start.12
  307.9 1.3 copy-start.16
  313.1 16.2 %all-to-all-start.16 = ((bf16[4,3,16,2304]{3,2,1,0:T(8,128)(2,1)}), bf16[4,3,16,2304]{3,2,1,0:T(8,128)(2,1)S(1)}, u32[]{:S(2)}, u32[]{:S(2)}) async-start(bf16[4,3,16,2304]{3,2,1,0:T(8,128)(2,1)} %shard_map.114), calls=%async_computation.16 | async-start | bytes 1769472 | tf_op jit(solution)/shard_map/all_to_all | solution.py:363
  330.1 15.8 %all-to-all-start.9 = ((bf16[8,1,48,512]{3,2,1,0:T(8,128)(2,1)}), bf16[8,1,48,512]{3,2,1,0:T(8,128)(2,1)}, u32[]{:S(2)}, u32[]{:S(2)}) async-start(bf16[8,1,48,512]{3,2,1,0:T(8,128)(2,1)} %shard_map.105), calls=%async_computation.9 | async-start | bytes 786432 | tf_op jit(solution)/shard_map/all_to_all | solution.py:360
  334.2 1.2 copy-start.24
  336.5 13.0 %copy-start.7 = (bf16[384,512]{1,0:T(8,128)(2,1)S(1)}, bf16[384,512]{1,0:T(8,128)(2,1)}, u32[]{:S(2)}) copy-start(bf16[384,512]{1,0:T(8,128)(2,1)} %constant.30.clone.table_ref) | copy-start | bytes 1179652
  345.9 32.1 %all-to-all-start.17 = ((bf16[8,3,48,512]{3,2,1,0:T(8,128)(2,1)}), bf16[8,3,48,512]{3,2,1,0:T(8,128)(2,1)S(1)}, u32[]{:S(2)}, u32[]{:S(2)}) async-start(bf16[8,3,48,512]{3,2,1,0:T(8,128)(2,1)} %copy-done.20), calls=%async_computation.17 | async-start | bytes 2359296 | tf_op jit(solution)/shard_map/all_to_all | solution.py:360
  (31 other events, 29.9 us)

commit v2 on v1

--- a/solution.py
+++ b/solution.py
@@ -262,84 +262,184 @@
         def body(field_ref, table_ref, out_ref):
             lines = jnp.swapaxes(field_ref[0], 0, 1).reshape(points, NX).astype(bf16)
             made = dot(table_ref[...], lines, ((1,), (1,))).astype(bf16)
-            out_ref[...] = made.reshape(cols, 1, 2 * kx_local, points)
+            out_ref[0] = made.reshape(cols, 2 * kx_local, points)
 
         return call(
             body,
             (count,),
             [pl.BlockSpec((1, rows_y, planes, NX), lambda i: (i, 0, 0, 0)), whole(tx_f)],
-            pl.BlockSpec((cols, 1, 2 * kx_local, points), lambda i: (0, i, 0, 0)),
-            jax.ShapeDtypeStruct((cols, count, 2 * kx_local, points), bf16),
+            pl.BlockSpec((1, cols, 2 * kx_local, points), lambda i: (i, 0, 0, 0)),
+            jax.ShapeDtypeStruct((count, cols, 2 * kx_local, points), bf16),
             COST * count,
             1 << 20,
         )(fields, tx_f)
 
-    def y_forward(incoming):
-        count = incoming.shape[1]
-
-        def body(in_ref, table_ref, out_ref):
-            lhs = jnp.concatenate(
-                [
-                    jnp.concatenate(
-                        [in_ref[c, 0, :, z * rows_y : (z + 1) * rows_y] for c in range(cols)], axis=1
-                    )
-                    for z in range(planes)
-                ],
-                axis=0,
+    def exchange(axis, size, src, dst, send, recv):
+        me = lax.axis_index(axis)
+
+        def copy(f, d):
+            peer = lax.rem(me + d, size)
+            return pltpu.make_async_remote_copy(
+                src_ref=src.at[f, peer],
+                dst_ref=dst.at[f, me],
+                send_sem=send.at[f, d - 1],
+                recv_sem=recv.at[f, d - 1],
+                device_id={axis: peer},
+                device_id_type=pl.DeviceIdType.MESH,
             )
-            made = dot(lhs, table_ref[...]).reshape(planes, 2 * kx_local, 2 * KY)
-            first, second = made[:, :kx_local], made[:, kx_local:]
-            real = jnp.swapaxes(first[:, :, :KY] + second[:, :, KY:], 0, 1)
-            imag = jnp.swapaxes(second[:, :, :KY] - first[:, :, KY:], 0, 1)
-            both = jnp.concatenate([real, imag], axis=1).astype(bf16)
-            for a in range(kx_local):
-                r, k = a // a_local, a % a_local
-                out_ref[r, 0, :, k * KY : (k + 1) * KY] = both[a]
+
+        def start(f):
+            for d in range(1, size):
+                copy(f, d).start()
+
+        def wait_recv(f):
+            for d in range(1, size):
+                copy(f, d).wait_recv()
+
+        def wait_send(f):
+            for d in range(1, size):
+                copy(f, d).wait_send()
+
+        def keep(f):
+            dst[f, me] = src[f, me]
+
+        return start, wait_recv, wait_send, keep
+
+    def greet():
+        barrier = pltpu.get_barrier_semaphore()
+        for axis, size in (("col", cols), ("row", rows)):
+            for d in range(1, size):
+                peer = lax.rem(lax.axis_index(axis) + d, size)
+                pl.semaphore_signal(
+                    barrier, inc=1, device_id={axis: peer}, device_id_type=pl.DeviceIdType.MESH
+                )
+        pl.semaphore_wait(barrier, cols + rows - 2)
+
+    def two_exchanges(incoming, table, first, second, compute, ident):
+        count = incoming.shape[0]
+        (axis1, size1, shape1), (axis2, size2, shape2) = first, second
+        ahead = 2
+
+        def body(in_ref, table_ref, out_ref, got, made, send1, recv1, send2, recv2):
+            greet()
+            start1, recv_1, sent1, keep1 = exchange(axis1, size1, in_ref, got, send1, recv1)
+            start2, recv_2, sent2, keep2 = exchange(axis2, size2, made, out_ref, send2, recv2)
+            for f in range(min(ahead, count)):
+                start1(f)
+
+            def step(f, carry):
+                @pl.when(f + ahead < count)
+                def _():
+                    start1(f + ahead)
+
+                keep1(f)
+                recv_1(f)
+                compute(f, got, table_ref, made)
+                start2(f)
+                keep2(f)
+                return carry
+
+            lax.fori_loop(0, count, step, 0)
+
+            def finish(f, carry):
+                recv_2(f)
+                sent1(f)
+                sent2(f)
+                return carry
+
+            lax.fori_loop(0, count, finish, 0)
+
+        sems = pltpu.SemaphoreType.DMA
+        return pl.pallas_call(
+            body,
+            in_specs=[pl.BlockSpec(memory_space=pltpu.VMEM)] * 2,
+            out_specs=pl.BlockSpec(memory_space=pltpu.VMEM),
+            out_shape=jax.ShapeDtypeStruct((count,) + shape2, bf16),
+            scratch_shapes=[
+                pltpu.VMEM((count,) + shape1, bf16),
+                pltpu.VMEM((count,) + shape2, bf16),
+                sems((count, size1 - 1)),
+                sems((count, size1 - 1)),
+                sems((count, size2 - 1)),
+                sems((count, size2 - 1)),
+            ],
+            compiler_params=pltpu.CompilerParams(
+                collective_id=ident, has_side_effects=True, vmem_limit_bytes=40 * 1024 * 1024
+            ),
+            cost_estimate=pl.CostEstimate(
+                flops=COST * count, bytes_accessed=1 << 20, transcendentals=0
+            ),
+        )(incoming, table)
+
+    col_side = ("col", cols, (cols, 2 * kx_local, points))
+    row_side = ("row", rows, (rows, 2 * planes, lanes))
+
+    def y_forward(f, in_ref, table_ref, out_ref):
+        lhs = jnp.concatenate(
+            [
+                jnp.concatenate(
+                    [in_ref[f, c, :, z * rows_y : (z + 1) * rows_y] for c in range(cols)], axis=1
+                )
+                for z in range(planes)
+            ],
+            axis=0,
+        )
+        made = dot(lhs, table_ref[...]).reshape(planes, 2 * kx_local, 2 * KY)
+        first, second = made[:, :kx_local], made[:, kx_local:]
+        real = jnp.swapaxes(first[:, :, :KY] + second[:, :, KY:], 0, 1)
+        imag = jnp.swapaxes(second[:, :, :KY] - first[:, :, KY:], 0, 1)
+        both = jnp.concatenate([real, imag], axis=1).astype(bf16)
+        for a in range(kx_local):
+            r, k = a // a_local, a % a_local
+            out_ref[f, r, :, k * KY : (k + 1) * KY] = both[a]
+
+    def y_inverse(f, in_ref, table_ref, out_ref):
+        lhs = jnp.concatenate(
+            [in_ref[f, r, :, k * KY : (k + 1) * KY] for r in range(rows) for k in range(a_local)],
+            axis=0,
+        )
+        made = dot(lhs, table_ref[...]).reshape(kx_local, 2 * planes, 2 * NY)
+        first, second = made[:, :planes], made[:, planes:]
+        real = jnp.swapaxes(first[:, :, :NY] - second[:, :, NY:], 0, 1)
+        imag = jnp.swapaxes(first[:, :, NY:] + second[:, :, :NY], 0, 1)
+        both = jnp.concatenate([real, imag], axis=1).astype(bf16)
+        for c in range(cols):
+            out_ref[f, c] = jnp.concatenate(
+                [both[z, :, c * rows_y : (c + 1) * rows_y] for z in range(planes)], axis=1
+            )
+
+    def to_spectral(x_lines, ident):
+        return two_exchanges(x_lines, ty_f, col_side, row_side, y_forward, ident)
+
+    def to_physical(z_lines, ident):
+        return two_exchanges(z_lines, ty_i, row_side, col_side, y_inverse, ident)
+
+    def x_forward_first():
+        def body(phase_ref, flow_ref, table_ref, out_ref):
+            i = pl.program_id(0)
+            c = phase_ref[...]
+            scalar = jnp.where(i == 0, c, c * c * c - c)
+            field = jnp.where((i == 0) | (i == 4), scalar, flow_ref[0])
+            lines = jnp.swapaxes(field, 0, 1).reshape(points, NX).astype(bf16)
+            made = dot(table_ref[...], lines, ((1,), (1,))).astype(bf16)
+            out_ref[0] = made.reshape(cols, 2 * kx_local, points)
 
         return call(
             body,
-            (count,),
-            [pl.BlockSpec((cols, 1, 2 * kx_local, points), lambda i: (0, i, 0, 0)), whole(ty_f)],
-            pl.BlockSpec((rows, 1, 2 * planes, lanes), lambda i: (0, i, 0, 0)),
-            jax.ShapeDtypeStruct((rows, count, 2 * planes, lanes), bf16),
-            COST * count,
+            (5,),
+            [
+                pl.BlockSpec((rows_y, planes, NX), lambda i: (0, 0, 0)),
+                pl.BlockSpec((1, rows_y, planes, NX), lambda i: (jnp.clip(i - 1, 0, 2), 0, 0, 0)),
+                whole(tx_f),
+            ],
+            pl.BlockSpec((1, cols, 2 * kx_local, points), lambda i: (i, 0, 0, 0)),
+            jax.ShapeDtypeStruct((5, cols, 2 * kx_local, points), bf16),
+            COST * 5,
             1 << 20,
-        )(incoming, ty_f)
-
-    def y_inverse(incoming):
-        count = incoming.shape[1]
-
-        def body(in_ref, table_ref, out_ref):
-            lhs = jnp.concatenate(
-                [
-                    in_ref[r, 0, :, k * KY : (k + 1) * KY]
-                    for r in range(rows)
-                    for k in range(a_local)
-                ],
-                axis=0,
-            )
-            made = dot(lhs, table_ref[...]).reshape(kx_local, 2 * planes, 2 * NY)
-            first, second = made[:, :planes], made[:, planes:]
-            real = jnp.swapaxes(first[:, :, :NY] - second[:, :, NY:], 0, 1)
-            imag = jnp.swapaxes(first[:, :, NY:] + second[:, :, :NY], 0, 1)
-            both = jnp.concatenate([real, imag], axis=1).astype(bf16)
-            for c in range(cols):
-                out_ref[c, 0] = jnp.concatenate(
-                    [both[z, :, c * rows_y : (c + 1) * rows_y] for z in range(planes)], axis=1
-                )
-
-        return call(
-            body,
-            (count,),
-            [pl.BlockSpec((rows, 1, 2 * planes, lanes), lambda i: (0, i, 0, 0)), whole(ty_i)],
-            pl.BlockSpec((cols, 1, 2 * kx_local, points), lambda i: (0, i, 0, 0)),
-            jax.ShapeDtypeStruct((cols, count, 2 * kx_local, points), bf16),
-            COST * count,
-            1 << 20,
-        )(incoming, ty_i)
+        )(phase, velocity, tx_f)
 
     def x_inverse(incoming):
-        count = incoming.shape[1]
+        count = incoming.shape[0]
 
         def body(in_ref, table_ref, out_ref):
             lines = in_ref[...].reshape(2 * KC, points)
@@ -349,24 +449,12 @@
         return call(
             body,
             (count,),
-            [pl.BlockSpec((cols, 1, 2 * kx_local, points), lambda i: (0, i, 0, 0)), whole(tx_i)],
+            [pl.BlockSpec((1, cols, 2 * kx_local, points), lambda i: (i, 0, 0, 0)), whole(tx_i)],
             pl.BlockSpec((1, rows_y, planes, NX), lambda i: (i, 0, 0, 0)),
             jax.ShapeDtypeStruct((count, rows_y, planes, NX), f32),
             COST * count,
             1 << 20,
         )(incoming, tx_i)
-
-    def over_col(values):
-        return lax.all_to_all(values, "col", split_axis=0, concat_axis=0, tiled=True)
-
-    def over_row(values):
-        return lax.all_to_all(values, "row", split_axis=0, concat_axis=0, tiled=True)
-
-    def forward(fields):
-        return over_row(y_forward(over_col(x_forward(fields))))
-
-    def inverse(outgoing):
-        return x_inverse(over_col(y_inverse(over_row(outgoing))))
 
     cut = KY
     steps = lanes // cut
@@ -376,14 +464,14 @@
     wave_xy = jnp.stack([wave_x, wave_y])
 
     def coefficient(in_ref, f, table_ref):
-        stacked = jnp.concatenate([in_ref[r, f] for r in range(rows)], axis=0)
+        stacked = jnp.concatenate([in_ref[f, r] for r in range(rows)], axis=0)
         return dot(table_ref[...], stacked) * scale_inv
 
     def emit(out_ref, f, real, imag, table_ref):
         both = jnp.concatenate([real, imag], axis=0).astype(bf16)
         made = dot(table_ref[...], both).astype(bf16)
         for r in range(rows):
-            out_ref[r, f] = made[r * 2 * planes : (r + 1) * 2 * planes]
+            out_ref[f, r] = made[r * 2 * planes : (r + 1) * 2 * planes]
 
     def waves(wave_ref):
         wx, wy = wave_ref[0:1, :], wave_ref[1:2, :]
@@ -392,105 +480,75 @@
         return wx, wy, wz, wx * wx + wy * wy + wz * wz
 
     def lines_spec(count):
-        return pl.BlockSpec((rows, count, 2 * planes, cut), lambda i: (0, 0, 0, i))
+        return pl.BlockSpec((count, rows, 2 * planes, cut), lambda i: (0, 0, 0, i))
 
     def coeff_spec(count):
         return pl.BlockSpec((count, 2 * modes_z, cut), lambda i: (0, 0, i))
 
     def lines_shape(count):
-        return jax.ShapeDtypeStruct((rows, count, 2 * planes, lanes), bf16)
+        return jax.ShapeDtypeStruct((count, rows, 2 * planes, lanes), bf16)
 
     def coeff_shape(count):
         return jax.ShapeDtypeStruct((count, 2 * modes_z, lanes), f32)
 
     wave_spec = pl.BlockSpec((2, cut), lambda i: (0, i))
 
-    def phase_spectral(in_ref, wave_ref, f_ref, i_ref, coeff_ref, out_ref):
+    def derive(in_ref, wave_ref, f_ref, i_ref, coeff_ref, out_ref):
         wx, wy, wz, k2 = waves(wave_ref)
-        c = coefficient(in_ref, 0, f_ref)
-        coeff_ref[0] = c
-        re, im = c[:modes_z], c[modes_z:]
-        emit(out_ref, 0, -(wx * im), wx * re, i_ref)
-        emit(out_ref, 1, -(wy * im), wy * re, i_ref)
-        emit(out_ref, 2, -(wz * im), wz * re, i_ref)
-        emit(out_ref, 3, -k2 * re, -k2 * im, i_ref)
-
-    def flow_spectral(in_ref, wave_ref, f_ref, i_ref, coeff_ref, out_ref):
-        wx, wy, wz, _ = waves(wave_ref)
-        cs = [coefficient(in_ref, j, f_ref) for j in range(3)]
-        for j in range(3):
+        cs = [coefficient(in_ref, j, f_ref) for j in range(5)]
+        for j in range(5):
             coeff_ref[j] = cs[j]
         re, im = [c[:modes_z] for c in cs], [c[modes_z:] for c in cs]
+        emit(out_ref, 0, -(wx * im[0]), wx * re[0], i_ref)
+        emit(out_ref, 1, -(wy * im[0]), wy * re[0], i_ref)
+        emit(out_ref, 2, -(wz * im[0]), wz * re[0], i_ref)
+        emit(out_ref, 3, -k2 * re[0], -k2 * im[0], i_ref)
         w = [wx, wy, wz]
         for j in range(3):
             p, q = (j + 1) % 3, (j + 2) % 3
-            emit(
-                out_ref,
-                j,
-                -(w[p] * im[q] - w[q] * im[p]),
-                w[p] * re[q] - w[q] * re[p],
-                i_ref,
-            )
-
-    def phase_solve(adv_ref, bulk_ref, old_ref, wave_ref, f_ref, i_ref, out_ref):
+            real = -(w[p] * im[1 + q] - w[q] * im[1 + p])
+            emit(out_ref, 4 + j, real, w[p] * re[1 + q] - w[q] * re[1 + p], i_ref)
+
+    def solve(in_ref, old_ref, wave_ref, f_ref, i_ref, out_ref):
         wx, wy, wz, k2 = waves(wave_ref)
-        adv = coefficient(adv_ref, 0, f_ref)
-        bulk = coefficient(bulk_ref, 0, f_ref)
-        old = old_ref[0]
         mean_mode = (wx == 0) & (wy == 0) & (wz == 0)
         stable = 1.0 / time_step + mobility * stabilizer * k2
         below = stable + mobility * epsilon * epsilon * k2 * k2
-        parts = []
-        for p in range(2):
-            at = slice(p * modes_z, (p + 1) * modes_z)
-            kept = jnp.where(mean_mode, 0.0, adv[at])
-            parts.append((stable * old[at] - kept - mobility * k2 * bulk[at]) / below)
-        emit(out_ref, 0, parts[0], parts[1], i_ref)
-
-    def flow_solve(force_ref, old_ref, wave_ref, f_ref, i_ref, out_ref):
-        wx, wy, wz, k2 = waves(wave_ref)
         viscous = 1.0 / time_step + k2 / reynolds
         largest = jnp.maximum(k2, 1.0)
         w = [wx, wy, wz]
-        force = [coefficient(force_ref, j, f_ref) for j in range(3)]
-        made = [[], [], []]
+        added = [coefficient(in_ref, j, f_ref) for j in range(4)]
+        made = [[], [], [], []]
         for p in range(2):
             at = slice(p * modes_z, (p + 1) * modes_z)
-            free = [(old_ref[j, at] / time_step + force[j][at]) / viscous for j in range(3)]
+            kept = jnp.where(mean_mode, 0.0, added[0][at])
+            made[0].append((stable * old_ref[0, at] - kept - mobility * k2 * old_ref[4, at]) / below)
+            free = [(old_ref[1 + j, at] / time_step + added[1 + j][at]) / viscous for j in range(3)]
             normal = (wx * free[0] + wy * free[1] + wz * free[2]) / largest
             for j in range(3):
-                made[j].append(free[j] - w[j] * normal)
-        for j in range(3):
+                made[1 + j].append(free[j] - w[j] * normal)
+        for j in range(4):
             emit(out_ref, j, made[j][0], made[j][1], i_ref)
 
-    phase_lines = forward(phase[None])
-    flow_lines = forward(velocity)
-    bulk_field = phase * phase * phase - phase
-    bulk_lines = forward(bulk_field[None])
     tail = [wave_spec, whole(tz_f), whole(tz_i)]
     last = (wave_xy, tz_f, tz_i)
-    coeff_phase, gradient_lines = call(
-        phase_spectral, (steps,), [lines_spec(1)] + tail,
-        [coeff_spec(1), lines_spec(4)], [coeff_shape(1), lines_shape(4)], COST, 1 << 20,
-    )(phase_lines, *last)
-    coeff_flow, vortex_lines = call(
-        flow_spectral, (steps,), [lines_spec(3)] + tail,
-        [coeff_spec(3), lines_spec(3)], [coeff_shape(3), lines_shape(3)], COST, 1 << 20,
-    )(flow_lines, *last)
-    leading = inverse(gradient_lines)
-    vortex = inverse(vortex_lines)
-    advect, _, potential = phase_terms(phase, velocity, leading[0:3], leading[3])
-    advect_lines = forward(advect[None])
-    force_lines = forward(momentum(velocity, vortex, leading[0:3], potential))
-    new_phase = call(
-        phase_solve, (steps,), [lines_spec(1), lines_spec(1), coeff_spec(1)] + tail,
-        lines_spec(1), lines_shape(1), COST, 1 << 20,
-    )(advect_lines, bulk_lines, coeff_phase, *last)
-    new_flow = call(
-        flow_solve, (steps,), [lines_spec(3), coeff_spec(3)] + tail,
-        lines_spec(3), lines_shape(3), COST, 1 << 20,
-    )(force_lines, coeff_flow, *last)
-    return (inverse(new_phase)[0], inverse(new_flow))
+    first_lines = to_spectral(x_forward_first(), 0)
+    coeffs, derived = call(
+        derive, (steps,), [lines_spec(5)] + tail,
+        [coeff_spec(5), lines_spec(7)], [coeff_shape(5), lines_shape(7)], COST, 1 << 20,
+    )(first_lines, *last)
+    fields = x_inverse(to_physical(derived, 1))
+    gradient, vortex = fields[0:3], fields[4:7]
+    advect, _, potential = phase_terms(phase, velocity, gradient, fields[3])
+    forcing = momentum(velocity, vortex, gradient, potential)
+    products = jnp.concatenate([advect[None], forcing], axis=0)
+    product_lines = to_spectral(x_forward(products), 2)
+    solved = call(
+        solve, (steps,), [lines_spec(4), coeff_spec(5)] + tail,
+        lines_spec(4), lines_shape(4), COST, 1 << 20,
+    )(product_lines, coeffs, *last)
+    result = x_inverse(to_physical(solved, 3))
+    return (result[0], result[1:4])
 
 
 def solution(mesh):

time: 384 us -> 240 us (0.62)
  waiting for transfers between devices: 190 us -> 0 us
  Pallas kernels: 56.4 us -> 227 us
  starting transfers between devices: 67.3 us -> 0 us
  local copies, waits for them, and re-layouts: 39.4 us -> 8.15 us
  blocking collectives: 19.1 us -> 0 us
  other arithmetic: 7.59 us -> 2.72 us
    all_to_all x17 -> x0, waiting for transfers between devices: 190 us -> none  [the longest x8 146 us: over_col(): lax.all_to_all(values, 'col', split_axis=0, concat_axis=0, tiled=True)]
    pallas_call x17 -> x9, Pallas kernels: 51.2 us -> 225 us  [the longest x4 210 us: two_exchanges(): pl.pallas_call(body, in_specs=[pl.BlockSpec(memory_space=pltpu.VMEM)] * 2...]
    all_to_all x17 -> x0, starting transfers between devices: 67.3 us -> none  [the longest x9 34.8 us: over_row(): lax.all_to_all(values, 'row', split_axis=0, concat_axis=0, tiled=True)]
    unnamed x95 -> x25, local copies, waits for them, and re-layouts: 39.4 us -> 5.14 us
    all_to_all x1 -> x0, blocking collectives: 19.1 us -> none  [over_col(): lax.all_to_all(values, 'col', split_axis=0, concat_axis=0, tiled=True)]
    another operation x2 -> x1, other arithmetic: 6.77 us -> 1.45 us  [momentum(): jnp.stack([velocity[1] * vortex[2] - velocity[2] * vortex[1] + potential...]
  transfers between devices with their start and end apart: 17 -> 0, of which waited for: 16 -> 0; matrix products, arithmetic and copies ran while one was open for 2% -> 0% of each run, Pallas kernels for 14% -> 0%
where the time goes in v2:
time: 240 us; the launch traced here: 239 us
  Pallas kernels  227 us (95%)
  local copies, waits for them, and re-layouts  8.15 us (3%)
  other arithmetic  2.72 us (1%)
    pallas_call x4, Pallas kernels, two_exchanges(): pl.pallas_call(body, in_specs=[pl.BlockSpec(memory_space=pltpu.VMEM)] * 2...  210 us
    pallas_call x2, Pallas kernels, x_inverse(): call(body, (count,), [pl.BlockSpec((1, cols, 2 * kx_local, points), lambd...  6.32 us
    unnamed x25, local copies, waits for them, and re-layouts  5.14 us

profile of v2, /device:TPU:0, one launch (start us, length us, event | category | flops | bytes accessed | tf_op | source)
XLA Modules:
  0.0 238.6 jit_solution(17588594351976200699)
XLA Ops:
  0.7 0.0 copy-start
  0.8 1.9 copy-done
  2.6 1.2 copy-done.3
  3.9 1.0 copy-done.5
  4.9 3.4 %shard_map.95.in_ref = bf16[5,8,48,512]{3,2,1,0:T(8,128)(2,1)S(1)} custom-call(f32[64,8,512]{2,1,0:T(8,128)S(1)} %copy-done.3, f32[3,64,8,512]{3,2,1,0:T(8,128)S(1)} %copy-done, bf16[384,512]{1,0:T(8,128)(2,1)S(1)} %copy-done.5), custom_call_target="tpu_custom_call" | custom-call | flops 2000000000 | bytes 1048576 | tf_op jit(solution)/shard_map/pallas_call | solution.py:427
  8.2 0.0 copy-done.10
  8.2 0.0 copy-start.7
  8.2 0.0 copy-start.8
  8.3 0.0 copy-start.9
  8.3 52.3 %shard_map.96.in_ref = bf16[5,4,16,2304]{3,2,1,0:T(8,128)(2,1)S(1)} custom-call(bf16[5,8,48,512]{3,2,1,0:T(8,128)(2,1)S(1)} %shard_map.95.in_ref, bf16[512,768]{1,0:T(8,128)(2,1)S(1)} %copy-done.10), custom_call_target="tpu_custom_call" | custom-call | flops 2000000000 | bytes 1048576 | tf_op jit(solution)/shard_map/pallas_call | solution.py:353
  60.6 0.0 copy-done.7
  60.6 0.0 copy-done.8
  60.6 2.8 %shard_map.97 = (f32[5,48,2304]{2,1,0:T(8,128)S(1)}, bf16[7,4,16,2304]{3,2,1,0:T(8,128)(2,1)S(1)}) custom-call(bf16[5,4,16,2304]{3,2,1,0:T(8,128)(2,1)S(1)} %shard_map.96.in_ref, f32[2,2304]{1,0:T(2,128)S(1)} %pad_maximum_fusion.1.wave_ref, bf16[48,64]{1,0:T(8,128)(2,1)S(1)} %copy-done.8, bf16[64,48]{1,0:T(8,128)(2,1)S(1)} %copy-done.7), custom_call_target="tpu_custom_call" | custom-call | flops 400000000 | bytes 1048576 | tf_op jit(solution)/shard_map/pallas_call | solution.py:536
  63.5 0.0 copy-start.2
  63.5 68.5 %shard_map.98.in_ref = bf16[7,8,48,512]{3,2,1,0:T(8,128)(2,1)S(1)} custom-call(bf16[7,4,16,2304]{3,2,1,0:T(8,128)(2,1)S(1)} %get-tuple-element.4.in_ref, bf16[384,1024]{1,0:T(8,128)(2,1)S(1)} %copy-done.9), custom_call_target="tpu_custom_call" | custom-call | flops 2800000000 | bytes 1048576 | tf_op jit(solution)/shard_map/pallas_call | solution.py:353
  132.0 0.0 copy-start.1
  132.0 4.0 %shard_map.99 = f32[7,64,8,512]{3,2,1,0:T(8,128)S(1)} custom-call(bf16[7,8,48,512]{3,2,1,0:T(8,128)(2,1)S(1)} %shard_map.98.in_ref, bf16[384,512]{1,0:T(8,128)(2,1)S(1)} %copy-done.2), custom_call_target="tpu_custom_call" | custom-call | flops 2800000000 | bytes 1048576 | tf_op jit(solution)/shard_map/pallas_call | solution.py:449
  136.1 0.0 copy-done.1
  136.1 0.0 copy-start.4
  136.1 0.8 multiply_add_fusion
  136.9 0.4 copy-done.4
  137.3 1.5 fusion.7
  138.7 0.0 copy-start.6
  138.8 0.4 pad_maximum_fusion.field_ref
  139.2 0.5 copy-done.6
  139.7 2.0 shard_map.100.in_ref
  141.7 44.9 %shard_map.101.in_ref = bf16[4,4,16,2304]{3,2,1,0:T(8,128)(2,1)S(1)} custom-call(bf16[4,8,48,512]{3,2,1,0:T(8,128)(2,1)S(1)} %shard_map.100.in_ref, bf16[512,768]{1,0:T(8,128)(2,1)S(1)} %copy-done.10), custom_call_target="tpu_custom_call" | custom-call | flops 1600000000 | bytes 1048576 | tf_op jit(solution)/shard_map/pallas_call | solution.py:353
  186.6 2.7 %shard_map.102.in_ref = bf16[4,4,16,2304]{3,2,1,0:T(8,128)(2,1)S(1)} custom-call(bf16[4,4,16,2304]{3,2,1,0:T(8,128)(2,1)S(1)} %shard_map.101.in_ref, f32[5,48,2304]{2,1,0:T(8,128)S(1)} %get-tuple-element.5.old_ref, f32[2,2304]{1,0:T(2,128)S(1)} %pad_maximum_fusion.1.wave_ref, bf16[48,64]{1,0:T(8,128)(2,1)S(1)} %copy-done.8, bf16[64,48]{1,0:T(8,128)(2,1)S(1)} %copy-done.7), custom_call_target="tpu_custom_call" | custom-call | flops 400000000 | bytes 1048576 | tf_op jit(solution)/shard_map/pallas_call | solution.py:546
  189.3 44.0 %shard_map.103.in_ref = bf16[4,8,48,512]{3,2,1,0:T(8,128)(2,1)S(1)} custom-call(bf16[4,4,16,2304]{3,2,1,0:T(8,128)(2,1)S(1)} %shard_map.102.in_ref, bf16[384,1024]{1,0:T(8,128)(2,1)S(1)} %copy-done.9), custom_call_target="tpu_custom_call" | custom-call | flops 1600000000 | bytes 1048576 | tf_op jit(solution)/shard_map/pallas_call | solution.py:353
  233.3 2.3 shard_map.104
  235.6 1.0 slice_bitcast_fusion
  236.7 2.0 slice.76
  (11 shorter events, 0.1 us)
Async XLA Ops:
  0.7 1.9 copy-start
  2.6 1.2 copy-start.3
  3.9 1.0 copy-start.5
  4.9 3.4 %copy-start.10 = (bf16[512,768]{1,0:T(8,128)(2,1)S(1)}, bf16[512,768]{1,0:T(8,128)(2,1)}, u32[]{:S(2)}) copy-start(bf16[512,768]{1,0:T(8,128)(2,1)} %constant.31.clone.table_ref) | copy-start | bytes 2359300
  8.2 52.4 %copy-start.7 = (bf16[64,48]{1,0:T(8,128)(2,1)S(1)}, bf16[64,48]{1,0:T(8,128)(2,1)}, u32[]{:S(2)}) copy-start(bf16[64,48]{1,0:T(8,128)(2,1)} %constant.34.clone.i_ref) | copy-start | bytes 18436
  8.2 52.4 %copy-start.8 = (bf16[48,64]{1,0:T(8,128)(2,1)S(1)}, bf16[48,64]{1,0:T(8,128)(2,1)}, u32[]{:S(2)}) copy-start(bf16[48,64]{1,0:T(8,128)(2,1)} %constant.33.clone.f_ref) | copy-start | bytes 18436
  8.3 55.2 %copy-start.9 = (bf16[384,1024]{1,0:T(8,128)(2,1)S(1)}, bf16[384,1024]{1,0:T(8,128)(2,1)}, u32[]{:S(2)}) copy-start(bf16[384,1024]{1,0:T(8,128)(2,1)} %constant.32.clone.table_ref) | copy-start | bytes 2359300
  63.5 68.5 %copy-start.2 = (bf16[384,512]{1,0:T(8,128)(2,1)S(1)}, bf16[384,512]{1,0:T(8,128)(2,1)}, u32[]{:S(2)}) copy-start(bf16[384,512]{1,0:T(8,128)(2,1)} %constant.30.clone.table_ref) | copy-start | bytes 1179652
  132.0 4.0 %copy-start.1 = (f32[3,64,8,512]{3,2,1,0:T(8,128)S(1)}, f32[3,64,8,512]{3,2,1,0:T(8,128)}, u32[]{:S(2)}) copy-start(f32[3,64,8,512]{3,2,1,0:T(8,128)} %flow_ref.1) | copy-start | bytes 9437188
  136.1 1.2 copy-start.4
  138.7 1.0 copy-start.6

commit v3 on v2

--- a/solution.py
+++ b/solution.py
@@ -256,24 +256,6 @@
     tx_f, tx_i, ty_f, ty_i, tz_f, tz_i = tables(cols, rows, rows_y, planes)
     f32, bf16 = jnp.float32, jnp.bfloat16
 
-    def x_forward(fields):
-        count = fields.shape[0]
-
-        def body(field_ref, table_ref, out_ref):
-            lines = jnp.swapaxes(field_ref[0], 0, 1).reshape(points, NX).astype(bf16)
-            made = dot(table_ref[...], lines, ((1,), (1,))).astype(bf16)
-            out_ref[0] = made.reshape(cols, 2 * kx_local, points)
-
-        return call(
-            body,
-            (count,),
-            [pl.BlockSpec((1, rows_y, planes, NX), lambda i: (i, 0, 0, 0)), whole(tx_f)],
-            pl.BlockSpec((1, cols, 2 * kx_local, points), lambda i: (i, 0, 0, 0)),
-            jax.ShapeDtypeStruct((count, cols, 2 * kx_local, points), bf16),
-            COST * count,
-            1 << 20,
-        )(fields, tx_f)
-
     def exchange(axis, size, src, dst, send, recv):
         me = lax.axis_index(axis)
 
@@ -315,26 +297,35 @@
                 )
         pl.semaphore_wait(barrier, cols + rows - 2)
 
-    def two_exchanges(incoming, table, first, second, compute, ident):
-        count = incoming.shape[0]
+    def two_exchanges(operands, count, first, second, prepare, compute, unfold, ident):
         (axis1, size1, shape1), (axis2, size2, shape2) = first, second
-        ahead = 2
-
-        def body(in_ref, table_ref, out_ref, got, made, send1, recv1, send2, recv2):
+        ins = len(operands)
+
+        def body(*refs):
+            in_refs, out_ref = refs[:ins], refs[ins]
+            got, made, send1, recv1, send2, recv2 = refs[ins + 1 : ins + 7]
+            more = list(refs[ins + 7 :])
+            source = more.pop(0) if prepare else in_refs[0]
+            landed = more.pop(0) if unfold else out_ref
+            start1, recv_1, sent1, keep1 = exchange(axis1, size1, source, got, send1, recv1)
+            start2, recv_2, sent2, keep2 = exchange(axis2, size2, made, landed, send2, recv2)
+            if prepare:
+                prepare(0, in_refs, source)
             greet()
-            start1, recv_1, sent1, keep1 = exchange(axis1, size1, in_ref, got, send1, recv1)
-            start2, recv_2, sent2, keep2 = exchange(axis2, size2, made, out_ref, send2, recv2)
-            for f in range(min(ahead, count)):
+            start1(0)
+
+            def begin(f, carry):
+                if prepare:
+                    prepare(f, in_refs, source)
                 start1(f)
+                return carry
+
+            lax.fori_loop(1, count, begin, 0)
 
             def step(f, carry):
-                @pl.when(f + ahead < count)
-                def _():
-                    start1(f + ahead)
-
                 keep1(f)
                 recv_1(f)
-                compute(f, got, table_ref, made)
+                compute(f, got, in_refs, made)
                 start2(f)
                 keep2(f)
                 return carry
@@ -343,6 +334,8 @@
 
             def finish(f, carry):
                 recv_2(f)
+                if unfold:
+                    unfold(f, landed, in_refs, out_ref)
                 sent1(f)
                 sent2(f)
                 return carry
@@ -350,31 +343,40 @@
             lax.fori_loop(0, count, finish, 0)
 
         sems = pltpu.SemaphoreType.DMA
+        scratch = [
+            pltpu.VMEM((count,) + shape1, bf16),
+            pltpu.VMEM((count,) + shape2, bf16),
+            sems((count, size1 - 1)),
+            sems((count, size1 - 1)),
+            sems((count, size2 - 1)),
+            sems((count, size2 - 1)),
+        ]
+        if prepare:
+            scratch.append(pltpu.VMEM((count,) + shape1, bf16))
+        if unfold:
+            scratch.append(pltpu.VMEM((count,) + shape2, bf16))
+            out_shape = jax.ShapeDtypeStruct((count, rows_y, planes, NX), f32)
+        else:
+            out_shape = jax.ShapeDtypeStruct((count,) + shape2, bf16)
         return pl.pallas_call(
             body,
-            in_specs=[pl.BlockSpec(memory_space=pltpu.VMEM)] * 2,
+            in_specs=[pl.BlockSpec(memory_space=pltpu.VMEM)] * ins,
             out_specs=pl.BlockSpec(memory_space=pltpu.VMEM),
-            out_shape=jax.ShapeDtypeStruct((count,) + shape2, bf16),
-            scratch_shapes=[
-                pltpu.VMEM((count,) + shape1, bf16),
-                pltpu.VMEM((count,) + shape2, bf16),
-                sems((count, size1 - 1)),
-                sems((count, size1 - 1)),
-                sems((count, size2 - 1)),
-                sems((count, size2 - 1)),
-            ],
+            out_shape=out_shape,
+            scratch_shapes=scratch,
             compiler_params=pltpu.CompilerParams(
                 collective_id=ident, has_side_effects=True, vmem_limit_bytes=40 * 1024 * 1024
             ),
             cost_estimate=pl.CostEstimate(
                 flops=COST * count, bytes_accessed=1 << 20, transcendentals=0
             ),
-        )(incoming, table)
+        )(*operands)
 
     col_side = ("col", cols, (cols, 2 * kx_local, points))
     row_side = ("row", rows, (rows, 2 * planes, lanes))
 
-    def y_forward(f, in_ref, table_ref, out_ref):
+    def y_forward(f, in_ref, in_refs, out_ref):
+        table_ref = in_refs[-1]
         lhs = jnp.concatenate(
             [
                 jnp.concatenate(
@@ -393,7 +395,8 @@
             r, k = a // a_local, a % a_local
             out_ref[f, r, :, k * KY : (k + 1) * KY] = both[a]
 
-    def y_inverse(f, in_ref, table_ref, out_ref):
+    def y_inverse(f, in_ref, in_refs, out_ref):
+        table_ref = in_refs[-1]
         lhs = jnp.concatenate(
             [in_ref[f, r, :, k * KY : (k + 1) * KY] for r in range(rows) for k in range(a_local)],
             axis=0,
@@ -408,48 +411,62 @@
                 [both[z, :, c * rows_y : (c + 1) * rows_y] for z in range(planes)], axis=1
             )
 
-    def to_spectral(x_lines, ident):
-        return two_exchanges(x_lines, ty_f, col_side, row_side, y_forward, ident)
-
-    def to_physical(z_lines, ident):
-        return two_exchanges(z_lines, ty_i, row_side, col_side, y_inverse, ident)
-
-    def x_forward_first():
-        def body(phase_ref, flow_ref, table_ref, out_ref):
-            i = pl.program_id(0)
-            c = phase_ref[...]
-            scalar = jnp.where(i == 0, c, c * c * c - c)
-            field = jnp.where((i == 0) | (i == 4), scalar, flow_ref[0])
-            lines = jnp.swapaxes(field, 0, 1).reshape(points, NX).astype(bf16)
-            made = dot(table_ref[...], lines, ((1,), (1,))).astype(bf16)
-            out_ref[0] = made.reshape(cols, 2 * kx_local, points)
-
-        return call(
-            body,
-            (5,),
-            [
-                pl.BlockSpec((rows_y, planes, NX), lambda i: (0, 0, 0)),
-                pl.BlockSpec((1, rows_y, planes, NX), lambda i: (jnp.clip(i - 1, 0, 2), 0, 0, 0)),
-                whole(tx_f),
-            ],
-            pl.BlockSpec((1, cols, 2 * kx_local, points), lambda i: (i, 0, 0, 0)),
-            jax.ShapeDtypeStruct((5, cols, 2 * kx_local, points), bf16),
-            COST * 5,
-            1 << 20,
-        )(phase, velocity, tx_f)
-
-    def x_inverse(incoming):
-        count = incoming.shape[0]
-
+    def x_lines(field, table_ref):
+        lines = jnp.swapaxes(field, 0, 1).reshape(points, NX).astype(bf16)
+        made = dot(table_ref[...], lines, ((1,), (1,))).astype(bf16)
+        return made.reshape(cols, 2 * kx_local, points)
+
+    def x_field(lines, table_ref):
+        made = dot(lines.reshape(2 * KC, points), table_ref[...], ((0,), (0,)))
+        return jnp.swapaxes(made.reshape(planes, rows_y, NX), 0, 1)
+
+    def first_to_spectral():
+        def prepare(f, in_refs, source):
+            phase_ref, flow_ref, table_ref, _ = in_refs
+            if isinstance(f, int):
+                source[f] = x_lines(phase_ref[...], table_ref)
+                return
+
+            @pl.when(f < 4)
+            def _():
+                source[f] = x_lines(flow_ref[jnp.minimum(f - 1, 2)], table_ref)
+
+            @pl.when(f == 4)
+            def _():
+                c = phase_ref[...]
+                source[f] = x_lines(c * c * c - c, table_ref)
+
+        operands = (phase, velocity, tx_f, ty_f)
+        return two_exchanges(operands, 5, col_side, row_side, prepare, y_forward, None, 0)
+
+    def products_to_spectral(products):
+        def prepare(f, in_refs, source):
+            source[f] = x_lines(in_refs[0][f], in_refs[1])
+
+        operands = (products, tx_f, ty_f)
+        return two_exchanges(operands, 4, col_side, row_side, prepare, y_forward, None, 2)
+
+    def derived_to_physical(derived):
+        def unfold(f, landed, in_refs, out_ref):
+            out_ref[f] = x_field(landed[f], in_refs[1])
+
+        operands = (derived, tx_i, ty_i)
+        return two_exchanges(operands, 7, row_side, col_side, None, y_inverse, unfold, 1)
+
+    def solved_to_lines(solved):
+        return two_exchanges((solved, ty_i), 4, row_side, col_side, None, y_inverse, None, 3)
+
+    def x_inverse(incoming, begin, count):
         def body(in_ref, table_ref, out_ref):
-            lines = in_ref[...].reshape(2 * KC, points)
-            made = dot(lines, table_ref[...], ((0,), (0,)))
-            out_ref[0] = jnp.swapaxes(made.reshape(planes, rows_y, NX), 0, 1)
+            out_ref[0] = x_field(in_ref[0], table_ref)
 
         return call(
             body,
             (count,),
-            [pl.BlockSpec((1, cols, 2 * kx_local, points), lambda i: (i, 0, 0, 0)), whole(tx_i)],
+            [
+                pl.BlockSpec((1, cols, 2 * kx_local, points), lambda i: (i + begin, 0, 0, 0)),
+                whole(tx_i),
+            ],
             pl.BlockSpec((1, rows_y, planes, NX), lambda i: (i, 0, 0, 0)),
             jax.ShapeDtypeStruct((count, rows_y, planes, NX), f32),
             COST * count,
@@ -532,23 +549,23 @@
 
     tail = [wave_spec, whole(tz_f), whole(tz_i)]
     last = (wave_xy, tz_f, tz_i)
-    first_lines = to_spectral(x_forward_first(), 0)
+    first_lines = first_to_spectral()
     coeffs, derived = call(
         derive, (steps,), [lines_spec(5)] + tail,
         [coeff_spec(5), lines_spec(7)], [coeff_shape(5), lines_shape(7)], COST, 1 << 20,
     )(first_lines, *last)
-    fields = x_inverse(to_physical(derived, 1))
+    fields = derived_to_physical(derived)
     gradient, vortex = fields[0:3], fields[4:7]
     advect, _, potential = phase_terms(phase, velocity, gradient, fields[3])
     forcing = momentum(velocity, vortex, gradient, potential)
     products = jnp.concatenate([advect[None], forcing], axis=0)
-    product_lines = to_spectral(x_forward(products), 2)
+    product_lines = products_to_spectral(products)
     solved = call(
         solve, (steps,), [lines_spec(4), coeff_spec(5)] + tail,
         lines_spec(4), lines_shape(4), COST, 1 << 20,
     )(product_lines, coeffs, *last)
-    result = x_inverse(to_physical(solved, 3))
-    return (result[0], result[1:4])
+    solved_lines = solved_to_lines(solved)
+    return (x_inverse(solved_lines, 0, 1)[0], x_inverse(solved_lines, 1, 3))
 
 
 def solution(mesh):

time: 240 us -> 232 us (0.967)
  Pallas kernels: 227 us -> 221 us
    pallas_call x6 -> x4, Pallas kernels: 215 us -> 211 us  [two_exchanges(): pl.pallas_call(body, in_specs=[pl.BlockSpec(memory_space=pltpu.VMEM)] * i...]
where the time goes in v3:
time: 232 us; the launch traced here: 231 us
  Pallas kernels  221 us (95%)
  local copies, waits for them, and re-layouts  5.96 us (3%)
  other arithmetic  2.8 us (1%)
    pallas_call x4, Pallas kernels, two_exchanges(): pl.pallas_call(body, in_specs=[pl.BlockSpec(memory_space=pltpu.VMEM)] * i...  211 us
    unnamed x25, local copies, waits for them, and re-layouts  5.96 us

profile of v3, /device:TPU:0, one launch (start us, length us, event | category | flops | bytes accessed | tf_op | source)
XLA Modules:
  0.0 230.9 jit_solution(3770467388052459865)
XLA Ops:
  0.6 0.0 copy-start.9
  0.6 0.0 copy-start.10
  0.8 0.0 copy-start
  0.8 1.9 copy-done
  2.7 0.0 copy-start.3
  2.7 1.2 copy-done.3
  3.9 0.0 copy-start.5
  3.9 1.1 copy-done.5
  5.0 0.0 copy-start.7
  5.0 1.0 copy-done.7
  6.0 0.0 copy-start.2
  6.0 52.7 %shard_map.95.in_ref = bf16[5,4,16,2304]{3,2,1,0:T(8,128)(2,1)S(1)} custom-call(f32[64,8,512]{2,1,0:T(8,128)S(1)} %copy-done.3, f32[3,64,8,512]{3,2,1,0:T(8,128)S(1)} %copy-done, bf16[384,512]{1,0:T(8,128)(2,1)S(1)} %copy-done.7, bf16[512,768]{1,0:T(8,128)(2,1)S(1)} %copy-done.5), custom_call_target="tpu_custom_call" | custom-call | flops 2000000000 | bytes 1048576 | tf_op jit(solution)/shard_map/pallas_call | solution.py:361
  58.8 0.0 copy-done.9
  58.8 0.0 copy-done.10
  58.8 2.8 %shard_map.96 = (f32[5,48,2304]{2,1,0:T(8,128)S(1)}, bf16[7,4,16,2304]{3,2,1,0:T(8,128)(2,1)S(1)}) custom-call(bf16[5,4,16,2304]{3,2,1,0:T(8,128)(2,1)S(1)} %shard_map.95.in_ref, f32[2,2304]{1,0:T(2,128)S(1)} %pad_maximum_fusion.1.wave_ref, bf16[48,64]{1,0:T(8,128)(2,1)S(1)} %copy-done.10, bf16[64,48]{1,0:T(8,128)(2,1)S(1)} %copy-done.9), custom_call_target="tpu_custom_call" | custom-call | flops 400000000 | bytes 1048576 | tf_op jit(solution)/shard_map/pallas_call | solution.py:553
  61.6 0.0 copy-done.2
  61.6 0.0 copy-done.4
  61.7 0.0 copy-start.1
  61.7 69.1 %shard_map.97 = f32[7,64,8,512]{3,2,1,0:T(8,128)S(1)} custom-call(bf16[7,4,16,2304]{3,2,1,0:T(8,128)(2,1)S(1)} %get-tuple-element.4.refs_0_, bf16[384,512]{1,0:T(8,128)(2,1)S(1)} %copy-done.2, bf16[384,1024]{1,0:T(8,128)(2,1)S(1)} %copy-done.4), custom_call_target="tpu_custom_call" | custom-call | flops 2800000000 | bytes 1048576 | tf_op jit(solution)/shard_map/pallas_call | solution.py:361
  130.8 0.0 copy-done.1
  130.8 0.8 multiply_add_fusion
  131.5 1.5 fusion.6
  133.0 0.0 copy-start.6
  133.0 0.0 copy-start.8
  133.0 0.5 pad_maximum_fusion.refs_0_
  133.6 0.6 copy-done.6
  134.1 0.1 copy-done.8
  134.2 45.3 %shard_map.98.in_ref = bf16[4,4,16,2304]{3,2,1,0:T(8,128)(2,1)S(1)} custom-call(f32[4,64,8,512]{3,2,1,0:T(8,128)S(1)} %pad_maximum_fusion.refs_0_, bf16[384,512]{1,0:T(8,128)(2,1)S(1)} %copy-done.8, bf16[512,768]{1,0:T(8,128)(2,1)S(1)} %copy-done.6), custom_call_target="tpu_custom_call" | custom-call | flops 1600000000 | bytes 1048576 | tf_op jit(solution)/shard_map/pallas_call | solution.py:361
  179.5 2.7 %shard_map.99.refs_0_ = bf16[4,4,16,2304]{3,2,1,0:T(8,128)(2,1)S(1)} custom-call(bf16[4,4,16,2304]{3,2,1,0:T(8,128)(2,1)S(1)} %shard_map.98.in_ref, f32[5,48,2304]{2,1,0:T(8,128)S(1)} %get-tuple-element.5.old_ref, f32[2,2304]{1,0:T(2,128)S(1)} %pad_maximum_fusion.1.wave_ref, bf16[48,64]{1,0:T(8,128)(2,1)S(1)} %copy-done.10, bf16[64,48]{1,0:T(8,128)(2,1)S(1)} %copy-done.9), custom_call_target="tpu_custom_call" | custom-call | flops 400000000 | bytes 1048576 | tf_op jit(solution)/shard_map/pallas_call | solution.py:563
  182.3 44.0 %shard_map.100.in_ref = bf16[4,8,48,512]{3,2,1,0:T(8,128)(2,1)S(1)} custom-call(bf16[4,4,16,2304]{3,2,1,0:T(8,128)(2,1)S(1)} %shard_map.99.refs_0_, bf16[384,1024]{1,0:T(8,128)(2,1)S(1)} %copy-done.4), custom_call_target="tpu_custom_call" | custom-call | flops 1600000000 | bytes 1048576 | tf_op jit(solution)/shard_map/pallas_call | solution.py:361
  226.3 1.5 shard_map.101
  227.8 3.1 %shard_map.102 = f32[3,64,8,512]{3,2,1,0:T(8,128)} custom-call(bf16[4,8,48,512]{3,2,1,0:T(8,128)(2,1)S(1)} %shard_map.100.in_ref, bf16[384,512]{1,0:T(8,128)(2,1)S(1)} %copy-done.2), custom_call_target="tpu_custom_call" | custom-call | flops 1200000000 | bytes 1048576 | tf_op jit(solution)/shard_map/pallas_call | solution.py:463
  (7 shorter events, 0.1 us)
Async XLA Ops:
  0.6 58.2 %copy-start.9 = (bf16[64,48]{1,0:T(8,128)(2,1)S(1)}, bf16[64,48]{1,0:T(8,128)(2,1)}, u32[]{:S(2)}) copy-start(bf16[64,48]{1,0:T(8,128)(2,1)} %constant.34.clone.i_ref) | copy-start | bytes 18436
  0.6 58.1 %copy-start.10 = (bf16[48,64]{1,0:T(8,128)(2,1)S(1)}, bf16[48,64]{1,0:T(8,128)(2,1)}, u32[]{:S(2)}) copy-start(bf16[48,64]{1,0:T(8,128)(2,1)} %constant.33.clone.f_ref) | copy-start | bytes 18436
  0.8 1.9 copy-start
  2.7 1.2 copy-start.3
  3.9 1.1 copy-start.5
  5.0 1.0 copy-start.7
  6.0 55.6 %copy-start.2 = (bf16[384,512]{1,0:T(8,128)(2,1)S(1)}, bf16[384,512]{1,0:T(8,128)(2,1)}, u32[]{:S(2)}) copy-start(bf16[384,512]{1,0:T(8,128)(2,1)} %constant.30.clone.refs_1_.table_ref) | copy-start | bytes 1179652
  6.0 55.6 %copy-start.4 = (bf16[384,1024]{1,0:T(8,128)(2,1)S(1)}, bf16[384,1024]{1,0:T(8,128)(2,1)}, u32[]{:S(2)}) copy-start(bf16[384,1024]{1,0:T(8,128)(2,1)} %constant.32.clone.refs_2_.refs_1_) | copy-start | bytes 2359300
  61.7 69.1 %copy-start.1 = (f32[3,64,8,512]{3,2,1,0:T(8,128)S(1)}, f32[3,64,8,512]{3,2,1,0:T(8,128)}, u32[]{:S(2)}) copy-start(f32[3,64,8,512]{3,2,1,0:T(8,128)} %refs_1_.4) | copy-start | bytes 9437188
  133.0 1.1 copy-start.6
  133.0 1.2 copy-start.8
